TPU v7x, 256 devices: a whole 4x4x8 slice. The times are simulated.
256 devices in a mesh: seq: 32 (over z, y), vocab: 8 (over x, core).
Axes of the slice: x: 4, y: 4, z: 8, core: 2. Of those that a mesh axis runs over, the one named last changes fastest.
Arguments:
- hidden: bfloat16 [3072, 3584], P('seq', 'vocab'), may hold values from -40 to 40
- lm_head: bfloat16 [3584, 152064], P(None, ('seq', 'vocab')), may hold values from -1 to 1
- positions: int32 [3072], replicated, may hold values from 0 to 3071, as said below
- vocab_limits: int32 [3072], replicated, may hold values from 76032 to 152064
- loss_mask: int32 [3072], P('seq'), may hold values 0 or 1
Outputs:
- token_entropy: float32 [3072], P('seq')
- mean_entropy: float32 [], replicated
Inputs may be any that keep to these rules, and one draw needn't show every extreme that they name: A permutation of the positions 0 to 3071: the response is cut into 64 blocks of 48 consecutive positions; rows i * 96 to i * 96 + 96 // 2 - 1 hold the positions of block i, the next 48 rows those of block 63 - i, in any order within a block.
All inputs are finite; a program needn't handle non-finite values. No bound on the sum of `loss_mask` on one device may be relied on, other than what follows from the above.
Results may differ from a plain program's by a relative error of at most 0.0003.
Values may be sent and summed in bfloat16 or wider, within the bound.
A program may use at most 128 MiB of HBM per device.

v0:
```python
import jax
import jax.numpy as jnp
from jax import lax
from jax.sharding import Mesh
from jax.sharding import PartitionSpec as P

SEQ_VOCAB = ("seq_0", "seq_1", "vocab_0", "vocab_1")
SEQ = ("seq_0", "seq_1")
VOCAB = ("vocab_0", "vocab_1")


masked_value = -1e30


def gather_axes(shard, axes, dim):
    whole = shard
    for number in range(len(axes) - 1, -1, -1):
        whole = lax.all_gather(whole, axes[number], axis=dim, tiled=True)
    return whole


def gathered_once(shard, axis):
    leaves = jax.tree.leaves(shard)
    order = sorted(range(len(leaves)), key=lambda k: -leaves[k].size)
    width = (1, *leaves[order[0]].shape)[-1]
    lines = [
        jnp.pad(leaves[k].reshape(-1), (0, -leaves[k].size % width)).reshape(-1, width)
        for k in order
    ]
    both, at, found = (lax.all_gather(jnp.concatenate(lines), axis), 0, {})
    for k, line in zip(order, lines):
        section = both[:, at : at + len(line)].reshape(len(both), -1)
        found[k] = section[:, : leaves[k].size].reshape(-1, *leaves[k].shape)
        at += len(line)
    numbers = iter(range(len(leaves)))
    return jax.tree.map(lambda _: found[next(numbers)], shard)


def combined_by_axis(shard, axes, combine):
    for axis in axes:
        pieces = gathered_once(shard, axis)
        shard = jax.tree.map(lambda part: part[0], pieces)
        for k in range(1, lax.axis_size(axis)):
            shard = combine(shard, jax.tree.map(lambda part: part[k], pieces))
    return shard


def copy_for_each(shard, axis):
    copies = jnp.broadcast_to(shard, (lax.axis_size(axis), *shard.shape))
    return lax.all_to_all(copies, axis, split_axis=0, concat_axis=0, tiled=True)


def taken_together(shard, axis):
    everything = copy_for_each(shard, axis)
    return jnp.sum(everything, axis=0)


def together(arrays, axis):
    flat, at, finished = (jnp.concatenate([a.reshape(-1) for a in arrays]), 0, [])
    total = taken_together(flat, axis)
    for a in arrays:
        finished.append(total[at : at + a.size].reshape(a.shape))
        at += a.size
    return tuple(finished)


def row_stats(logits, row_limits, first_column):
    columns = first_column + lax.iota(jnp.int32, logits.shape[1])
    allowed = columns[None, :] < row_limits[:, None]
    row_peak = jnp.max(jnp.where(allowed, logits, masked_value), axis=1)
    shifted = logits - row_peak[:, None]
    weights = jnp.where(allowed, jnp.exp(shifted), 0.0)
    row_total = jnp.sum(weights, axis=1)
    row_moment = jnp.sum(weights * jnp.where(allowed, shifted, 0.0), axis=1)
    return (row_peak, row_total, row_moment)


def combine_stats(first, second):
    peak_one, total_one, moment_one = first
    peak_two, total_two, moment_two = second
    shared = jnp.maximum(peak_one, peak_two)
    ratio_one = jnp.exp(peak_one - shared)
    ratio_two = jnp.exp(peak_two - shared)
    total = ratio_one * total_one + ratio_two * total_two
    moment = ratio_one * (moment_one + total_one * (peak_one - shared)) + ratio_two * (
        moment_two + total_two * (peak_two - shared)
    )
    return (shared, total, moment)


def local(hidden, lm_head, positions, vocab_limits, loss_mask):
    tok_dev = hidden.shape[0]
    width_dev = lm_head.shape[1]
    tokens_all = positions.shape[0]
    first_column = lax.axis_index(SEQ_VOCAB) * width_dev
    all_tokens = gather_axes(hidden, SEQ, 0)
    logits = jnp.dot(
        lax.all_gather(all_tokens, VOCAB, axis=1, tiled=True),
        lm_head,
        preferred_element_type=jnp.float32,
    )
    stats = row_stats(logits, vocab_limits, first_column)
    own_start = lax.axis_index(SEQ) * tok_dev
    row_peak, row_total, row_moment = combined_by_axis(stats, SEQ_VOCAB, combine_stats)
    entropy_rows = jnp.log(row_total) - row_moment / row_total
    arranged = jnp.zeros((tokens_all,), jnp.float32).at[positions].set(entropy_rows)
    token_entropy = lax.dynamic_slice_in_dim(arranged, own_start, tok_dev)
    mask_float = loss_mask.astype(jnp.float32)
    masked_sum, mask_count = together(
        (jnp.sum(token_entropy * mask_float), jnp.sum(mask_float)), SEQ
    )
    mean_entropy = masked_sum / jnp.maximum(mask_count, 1.0)
    return (token_entropy, mean_entropy)


def solution(mesh):
    torus = Mesh(mesh.devices.reshape(8, 4, 4, 2), ("seq_0", "seq_1", "vocab_0", "vocab_1"))
    in_specs = (P(SEQ, VOCAB), P(None, SEQ_VOCAB), P(), P(), P(SEQ))
    out_specs = (P(SEQ), P())
    return jax.shard_map(local, mesh=torus, in_specs=in_specs, out_specs=out_specs, check_vma=False)
```

profile of v0, /device:TPU:1, one launch (start us, length us, event | category | flops | bytes accessed | tf_op | source)
XLA Modules:
  0.0 298.8 jit_solution(5486878715596462331)
XLA Ops:
  7.2 0.0 copy-start.1
  7.2 0.0 copy-start
  7.2 0.0 all-gather.11.cloned.1.call-start
  7.2 13.0 %all_gather.33 = bf16[384,448]{1,0:T(8,128)(2,1)} all-gather(bf16[96,448]{1,0:T(8,128)(2,1)} %param.5), channel_id=1, replica_groups=mesh['seq_0'=8,'seq_1'=4,'vocab_0'=4,'vocab_1'=2] {'seq_1'}, dimensions={0}, use_global_device_ids=true | all-gather | bytes 430080 | tf_op jit(solution)/shard_map/all_gather | solution.py:18
  20.2 0.0 all-gather.11.cloned.1.call-update
  20.3 0.0 all-gather.13.cloned.1.call-start
  20.3 48.6 %all-gather.11.cloned.1.call-done = bf16[3072,448]{1,0:T(8,128)(2,1)} async-done(((bf16[384,448]{1,0:T(8,128)(2,1)}), bf16[3072,448]{1,0:T(8,128)(2,1)}) %all-gather.11.cloned.1.call-update) | async-done | bytes 2752528 | tf_op jit(solution)/shard_map/all_gather | solution.py:18
  68.9 4.6 %copy.10 = bf16[3072,448]{0,1:T(8,128)(2,1)} copy(bf16[3072,448]{1,0:T(8,128)(2,1)} %all-gather.11.cloned.1.call-done) | data formatting | bytes 5505024 | tf_op jit(solution)/shard_map/all_gather | solution.py:18
  73.5 0.0 all-gather.13.cloned.1.call-update
  73.6 0.0 copy-done.1
  73.6 109.1 %all-gather.13.cloned.1.call-done = bf16[3072,3584]{0,1:T(8,128)(2,1)} async-done(((bf16[3072,448]{0,1:T(8,128)(2,1)}), bf16[3072,3584]{0,1:T(8,128)(2,1)}) %all-gather.13.cloned.1.call-update) | async-done | bytes 22020112 | tf_op jit(solution)/shard_map/all_gather | solution.py:98
  182.8 0.0 copy-done
  182.8 18.4 %fusion = (f32[3072]{0:T(1024)S(1)}, f32[3072,594]{0,1:T(8,128)S(1)}) fusion(s32[3072]{0:T(1024)S(1)} %copy-done, s32[594]{0:T(1024)S(1)} %iota_add_fusion, bf16[3072,3584]{0,1:T(8,128)(2,1)} %all-gather.13.cloned.1.call-done, bf16[3584,594]{0,1:T(8,128)(2,1)} %param.6), kind=kOutput, calls=%fused_computation.4 | convolution fusion | flops 13085408256 | bytes 33603912 | tf_op jit(solution)/shard_map/dot_general | solution.py:97
  201.2 0.0 copy-start.2
  201.2 2.5 fusion.3
  203.8 20.1 %all-gather.4 = f32[8,3,3072]{2,1,0:T(4,128)S(1)} all-gather(f32[1,3,3072]{2,1,0:T(4,128)S(1)} %maximum_bitcast_fusion), channel_id=2, replica_groups=mesh['seq_0'=8,'seq_1'=4,'vocab_0'=4,'vocab_1'=2] {'seq_0'}, dimensions={0}, use_global_device_ids=true | all-gather | bytes 331776 | tf_op jit(solution)/shard_map/all_gather | solution.py:30
  223.9 0.1 fusion.63
  224.0 0.3 multiply_add_fusion.6
  224.3 0.5 fusion.28
  224.8 9.9 %all-gather.5 = f32[4,3,3072]{2,1,0:T(4,128)S(1)} all-gather(f32[1,3,3072]{2,1,0:T(4,128)S(1)} %maximum_bitcast_fusion.1), channel_id=3, replica_groups=mesh['seq_0'=8,'seq_1'=4,'vocab_0'=4,'vocab_1'=2] {'seq_1'}, dimensions={0}, use_global_device_ids=true | all-gather | bytes 184320 | tf_op jit(solution)/shard_map/all_gather | solution.py:30
  234.6 0.1 fusion.70
  234.8 0.2 fusion.17
  235.0 9.2 %all-gather.6 = f32[4,3,3072]{2,1,0:T(4,128)S(1)} all-gather(f32[1,3,3072]{2,1,0:T(4,128)S(1)} %maximum_bitcast_fusion.2), channel_id=4, replica_groups=mesh['seq_0'=8,'seq_1'=4,'vocab_0'=4,'vocab_1'=2] {'vocab_0'}, dimensions={0}, use_global_device_ids=true | all-gather | bytes 184320 | tf_op jit(solution)/shard_map/all_gather | solution.py:30
  244.3 0.1 fusion.77
  244.4 0.2 fusion.6
  244.7 13.7 %all-gather.7 = f32[2,3,3072]{2,1,0:T(4,128)S(1)} all-gather(f32[1,3,3072]{2,1,0:T(4,128)S(1)} %maximum_bitcast_fusion.3), channel_id=5, replica_groups=mesh['seq_0'=8,'seq_1'=4,'vocab_0'=4,'vocab_1'=2] {'vocab_1'}, dimensions={0}, use_global_device_ids=true | all-gather | bytes 110592 | tf_op jit(solution)/shard_map/all_gather | solution.py:30
  258.4 0.1 fusion.82
  258.5 11.8 %scatter_custom_fusion = f32[3072]{0:T(1024)S(1)} fusion(s32[3072]{0:T(1024)S(1)} %compare_select_fusion.3, f32[3072]{0:T(1024)S(1)} %divide_subtract_fusion, f32[]{:T(128)} %constant.16.clone.1), kind=kCustom, calls=%fused_computation.151 | custom fusion | bytes 12292 | tf_op jit(solution)/shard_map/scatter | solution.py:106
  270.3 0.0 copy-done.2
  270.3 1.3 multiply_reduce_fusion
  271.5 1.4 pad_maximum_fusion
  273.0 15.9 %all_to_all.6 = f32[32,1,2]{2,1,0:T(1,128)S(1)} all-to-all(f32[32,1,2]{2,1,0:T(1,128)S(1)} %broadcast_in_dim.24), channel_id=1, replica_groups=mesh['seq_0'=8,'seq_1'=4,'vocab_0'=4,'vocab_1'=2] {'seq_0','seq_1'}, dimensions={0} | all-to-all | bytes 512 | tf_op jit(solution)/shard_map/all_to_all | solution.py:50
  288.8 0.1 reduce_sum.49
  288.9 0.6 fusion.83
  (8 shorter events, 0.2 us)
Async XLA Ops:
  7.2 66.4 %copy-start.1 = (s32[3072]{0:T(1024)S(1)}, s32[3072]{0:T(1024)}, u32[]{:S(2)}) copy-start(s32[3072]{0:T(1024)} %param.7) | copy-start | bytes 36868
  7.2 175.6 %copy-start = (s32[3072]{0:T(1024)S(1)}, s32[3072]{0:T(1024)}, u32[]{:S(2)}) copy-start(s32[3072]{0:T(1024)} %param.8) | copy-start | bytes 36868
  7.2 61.7 %all-gather.11.cloned.1.call-start = ((), (), s32[]{:S(2)}) async-start(), calls=%async_computation.1 | async-start | bytes 3538944 | tf_op jit(solution)/shard_map/all_gather | solution.py:18
  20.3 162.5 %all-gather.13.cloned.1.call-start = ((), (), s32[]{:S(2)}) async-start(), calls=%async_computation.2 | async-start | bytes 24772608 | tf_op jit(solution)/shard_map/all_gather | solution.py:98
  201.2 69.1 %copy-start.2 = (s32[96]{0:T(128)S(1)}, s32[96]{0:T(128)}, u32[]{:S(2)}) copy-start(s32[96]{0:T(128)} %param.9) | copy-start | bytes 1156
Sparse Core Ops, SparseCore 0:
  20.4 48.4 all-gather.10
  73.7 109.0 all-gather.12
where the time goes:
time: 299 us
  waiting for transfers between devices  158 us (53%)
  blocking collectives  81.8 us (27%)
  matrix products  18.4 us (6%)
  local copies, waits for them, and re-layouts  17.1 us (6%)
  between operations  16.7 us (6%)
  other arithmetic  6.95 us (2%)
    all_gather x1, waiting for transfers between devices, local(): lax.all_gather(all_tokens, VOCAB, axis=1, tiled=True)  109 us
    all_gather x4, blocking collectives, gathered_once(): both, at, found = (lax.all_gather(jnp.concatenate(lines), axis), 0, {})  53 us
    all_gather x1, waiting for transfers between devices, gather_axes(): whole = lax.all_gather(whole, axes[number], axis=dim, tiled=True)  48.6 us
    dot_general x1, matrix products, local(): jnp.dot(lax.all_gather(all_tokens, VOCAB, axis=1, tiled=True), lm_head, p...  18.4 us
    all_to_all x1, blocking collectives, copy_for_each(): return lax.all_to_all(copies, axis, split_axis=0, concat_axis=0, tiled=True)  15.9 us
    all_gather x1, blocking collectives, gather_axes(): whole = lax.all_gather(whole, axes[number], axis=dim, tiled=True)  13 us
    scatter x1, local copies, waits for them, and re-layouts, local(): jnp.zeros((tokens_all,), jnp.float32).at[positions].set(entropy_rows)  11.8 us
  transfers between devices with their start and end apart: 2, of which 2 were waited for; matrix products, arithmetic and copies ran while one was open for 0% of the time, Pallas kernels for 0%

commit v1 on v0

v1 whole, which is shorter than its diff:
```python
import heapq

import jax
import jax.numpy as jnp
from jax import lax
from jax.experimental import pallas as pl
from jax.experimental.pallas import tpu as pltpu
from jax.sharding import Mesh
from jax.sharding import PartitionSpec as P

NZ, NY, NX = 8, 4, 4
SIZE = {"z": NZ, "y": NY, "x": NX}
AXES = ("z", "y", "x", "c")
MESH = pl.DeviceIdType.MESH
HALF, RB, COLORS = 48, 16, 3
TOK = 96
ROWS = NY * HALF
D, FEAT = 3584, 896
WID, SLOT = 594, 640
COLS = 2 * SLOT
TILE = 256
NEG = -1e30
ORDER = (0, 1, 7, 2, 6, 3, 5, 4)
DEADLINE = (8.7, 7.5, 14.8, 17.9, 19.6)
UNIT, HOP, BACKLOG = 0.615, 1.75, 2.0
WINDOW = 2.9


def onward(n, d, far):
    if d == 0:
        return [1, -1]
    if d < n // 2:
        return [-1] if d + 1 < n // 2 or far == -1 else []
    if d > n // 2:
        return [1] if d - 1 > n // 2 or far == 1 else []
    return []


def parity(k):
    return 1 if k % 2 == 0 else -1


def sends_of(p):
    color, axis, rest = p[0], p[1], p[2:]
    out = []
    if color == "A" and axis == "y":
        (dy,) = rest
        out += [("y", m, 1, ("A", "y", (dy - m) % 4)) for m in onward(4, dy, 1)]
        out += [("x", m, 1, ("A", "x", dy, -m % 4)) for m in (1, -1)]
    elif color == "A" and axis == "x":
        dy, dx = rest
        out += [("x", m, 1, ("A", "x", dy, (dx - m) % 4)) for m in onward(4, dx, parity(dy))]
    elif color == "A":
        dz, dy = rest
        out += [("z", m, 4, ("A", "z", (dz - m) % 8, dy)) for m in onward(8, dz, parity(dy))]
    elif axis == "z":
        (dz,) = rest
        far = 1 if color == "B" else -1
        out += [("z", m, 1, (color, "z", (dz - m) % 8)) for m in onward(8, dz, far)]
        second = "y" if color == "B" else "x"
        out += [(second, m, 1, (color, second, dz, -m % 4)) for m in (1, -1)]
    else:
        dz, d = rest
        last = (color, axis) in (("B", "x"), ("C", "y"))
        size = 4 if last else 1
        out += [(axis, m, size, (color, axis, dz, (d - m) % 4)) for m in onward(4, d, parity(dz))]
    return out


def launch_of(p):
    color, axis = p[0], p[1]
    if color == "A" and axis != "z":
        return ("A", "z", 0, p[2])
    if color == "B" and axis != "x":
        return ("B", "x", p[2], 0)
    if color == "C" and axis != "y":
        return ("C", "y", p[2], 0)
    return None


def parts_of(launch):
    color, _, a, b = launch
    if color == "A":
        return [("A", "y", b)] + [("A", "x", b, k) for k in (1, 2, 3)]
    if color == "B":
        return [("B", "z", a)] + [("B", "y", a, k) for k in (1, 2, 3)]
    return [("C", "z", a)] + [("C", "x", a, k) for k in (1, 2, 3)]


def window_of(p):
    return 0 if p[0] == "A" and p[1] != "z" else p[2]


def pieces_of_window(dz):
    need = [("B", "x", dz, k) for k in range(4)] + [("C", "y", dz, k) for k in range(4)]
    return need + [("A", "z", dz, k) for k in range(4)]


def plan(preps):
    due = {}

    def latest(p):
        if p not in due:
            dz = window_of(p)
            k = DEADLINE[min(dz, 8 - dz)]
            ahead = sends_of(p)
            launch = launch_of(p)
            if launch:
                ahead = ahead + sends_of(launch)
            for _, _, size, q in ahead:
                k = min(k, latest(q) - HOP - size * UNIT - 0.3)
            due[p] = k
        return due[p]

    free = {(a, m): 0.0 for a in "xyz" for m in (1, -1)}
    waiting = {k: [] for k in free}
    have, steps, flying = set(), [], []
    count = 0
    now = 0.0

    def offer(sends):
        nonlocal count
        for axis, m, size, q in sends:
            heapq.heappush(waiting[axis, m], (latest(q) - size * UNIT, count, size, q))
            count += 1

    def pump():
        nonlocal count
        for link in free:
            while waiting[link] and free[link] - now < BACKLOG:
                _, _, size, q = heapq.heappop(waiting[link])
                free[link] = max(free[link], now) + size * UNIT
                heapq.heappush(flying, (free[link] + HOP, count, q))
                count += 1
                steps.append(("send", link[0], link[1], q))

    def take(p):
        have.add(p)
        offer(sends_of(p))
        launch = launch_of(p)
        if launch and launch not in have and all(q in have for q in parts_of(launch)):
            have.add(launch)
            offer(sends_of(launch))

    for p in (("A", "y", 0), ("B", "z", 0), ("C", "z", 0)):
        take(p)
    pump()
    left = list(ORDER)
    preps = list(preps)
    while flying or left:
        if flying and flying[0][0] <= now:
            _, _, q = heapq.heappop(flying)
            steps.append(("wait", q))
            take(q)
            pump()
            now += 0.03
            continue
        if preps and now >= preps[0][1]:
            name, _, cost = preps.pop(0)
            steps.append(("prep", name))
            now += cost
            pump()
            continue
        ready = [] if preps else [w for w in left if all(q in have for q in pieces_of_window(w))]
        if ready:
            left.remove(ready[0])
            steps.append(("window", ready[0]))
            now += WINDOW
            pump()
            continue
        nxt = [flying[0][0]] if flying else []
        if preps:
            nxt.append(preps[0][1])
        now = max(now, min(nxt))
    return steps


PREPS = (
    [(("limits", k), 0.2, 0.45) for k in range(6)]
    + [(("places", 0), 3.0, 0.4)]
    + [(("own", k), 4.0, 0.3) for k in range(2)]
    + [(("other", k), 11.0, 0.3) for k in range(2)]
    + [(("mask", 0), 12.0, 0.1), (("mask", 1), 17.0, 0.1)]
)
STEPS = plan(PREPS)
TRANSFERS = [s[3] for s in STEPS if s[0] == "send"]
NUMBER = {q: k for k, q in enumerate(TRANSFERS)}


def merge(parts):
    peak = parts[0][0]
    for p in parts[1:]:
        peak = jnp.maximum(peak, p[0])
    total = jnp.zeros_like(peak)
    moment = jnp.zeros_like(peak)
    for m, t, mo in parts:
        shift = m - peak
        ratio = jnp.exp(shift)
        total = total + ratio * t
        moment = moment + ratio * (mo + t * shift)
    return peak, total, moment


def kernel(hid_ref, lm_ref, pos_ref, lim_ref, mask_ref, ent_ref, mean_ref,
           held, weight, stage, hstage, pstage, logits, turned, lim_col, pos_col, cols,
           slab, stat, from_z, plane, from_plane, ents, masks,
           send_sem, recv_sem, hx_sem, w_sem, mz_sem, my_sem, rz_sem, rp_sem, re_sem, copy_sem):
    z, y, x, c = (lax.axis_index(a) for a in AXES)
    here = {"z": z, "y": y, "x": x, "c": c}

    def device(**moved):
        return tuple(lax.rem(here[a] + moved[a], SIZE[a]) if a in moved and a != "c" else
                     (1 - c if a in moved else here[a]) for a in AXES)

    own_w = pltpu.make_async_copy(lm_ref, stage.at[0], copy_sem.at[0])
    own_h = pltpu.make_async_copy(hid_ref, hstage, copy_sem.at[1])
    own_h.start()
    own_w.start()

    barrier = pltpu.get_barrier_semaphore()
    near = [device(**{a: d}) for a in "zyx" for d in (1, SIZE[a] - 1)] + [device(c=1)]
    for who in near:
        pl.semaphore_signal(barrier, inc=1, device_id=who, device_id_type=MESH)
    pl.semaphore_wait(barrier, len(near))

    own_h.wait()
    swap = pltpu.make_async_remote_copy(
        src_ref=hstage.at[pl.ds(pl.multiple_of((1 - c) * HALF, RB), HALF), :], dst_ref=pstage,
        send_sem=hx_sem.at[0], recv_sem=hx_sem.at[1], device_id=device(c=1), device_id_type=MESH)
    swap.start()
    give_w = pltpu.make_async_remote_copy(
        src_ref=lm_ref, dst_ref=stage.at[1],
        send_sem=w_sem.at[0], recv_sem=w_sem.at[1], device_id=device(c=1), device_id_type=MESH)

    def feature(dx):
        return pl.ds(pl.multiple_of(lax.rem(x + dx, NX) * FEAT, 128), FEAT)

    mine = hstage[pl.ds(pl.multiple_of(c * HALF, RB), HALF), :].astype(jnp.float32)
    swap.wait_recv()
    theirs = pstage[...].astype(jnp.float32)
    first = c == 0
    left = jnp.where(first, mine, theirs)
    right = jnp.where(first, theirs, mine)
    both = jnp.concatenate([left, right], axis=1).astype(jnp.bfloat16)
    for k in range(COLORS):
        held[0, 0, k, :, feature(0)] = both[k * RB:(k + 1) * RB]

    def place(p):
        color, axis = p[0], p[1]
        if color == "A":
            if axis == "z":
                return held.at[p[2], p[3], 0]
            return held.at[0, p[2], 0, :, feature(0 if axis == "y" else p[3])]
        if axis == "z":
            return held.at[p[2], 0, 1 if color == "B" else 2, :, feature(0)]
        if color == "B":
            if axis == "y":
                return held.at[p[2], p[3], 1, :, feature(0)]
            return held.at[p[2], :, 1, :, feature(p[3])]
        if axis == "x":
            return held.at[p[2], 0, 2, :, feature(p[3])]
        return held.at[p[2], p[3], 2]

    def transfer(q, axis, m):
        k = NUMBER[q]
        n = SIZE[axis]
        if axis == "x":
            source = q[:-1] + ((q[-1] + m) % n,)
        else:
            at = {("A", "y"): 2, ("A", "z"): 2, ("B", "z"): 2, ("C", "z"): 2}.get(q[:2], 3)
            source = q[:at] + ((q[at] + m) % n,) + q[at + 1:]
        if (q[0], axis) in (("A", "x"), ("B", "y"), ("C", "x")) and source[3] == 0:
            source = (q[0], "y" if q[0] == "A" else "z", q[2])
        dst = place(q)
        if axis == "x":
            src = dst_at = None
            column = feature(q[-1] + m + NX)
            if q[0] == "A":
                src = dst_at = held.at[0, q[2], 0, :, column]
            elif q[0] == "B":
                src = dst_at = held.at[q[2], :, 1, :, column]
            else:
                src = dst_at = held.at[q[2], 0, 2, :, column]
            dst = dst_at
        else:
            src = place(source)
        return pltpu.make_async_remote_copy(
            src_ref=src, dst_ref=dst, send_sem=send_sem.at[k], recv_sem=recv_sem.at[k],
            device_id=device(**{axis: m % n}), device_id_type=MESH)

    started = {}
    lanes = lax.broadcasted_iota(jnp.int32, (128, 128), 1)

    def limits(k):
        if k == 0:
            pad = jnp.zeros((128 - 24, 128), jnp.float32)
            turned[0] = jnp.concatenate([lim_ref[...].astype(jnp.float32), pad], axis=0).T
            turned[1] = jnp.concatenate([pos_ref[...].astype(jnp.float32), pad], axis=0).T
            j = lax.broadcasted_iota(jnp.int32, (1, COLS), 1)
            number = (z * NY + y) * (2 * NX) + x * 2
            start = jnp.where(j < SLOT, (number + c) * WID, (number + 1 - c) * WID - SLOT)
            inside = jnp.where(j < SLOT, j, j - SLOT) < WID
            cols[...] = jnp.where(inside, start + j, 1 << 28).astype(jnp.float32)

        def one(r, carry):
            column = jnp.sum(jnp.where(lanes == r, turned[0], 0.0), axis=1, keepdims=True)
            lim_col[pl.ds(pl.multiple_of(r * 128, 128), 128), :] = jnp.broadcast_to(column, (128, 128))
            return carry

        lax.fori_loop(4 * k, 4 * k + 4, one, 0)

    def places():
        for k in range(3):
            column = jnp.sum(jnp.where(lanes == 3 * z + k, turned[1], 0.0), axis=1, keepdims=True)
            pos_col[k * 128:(k + 1) * 128, :] = jnp.broadcast_to(column, (128, 128))
        slab[...] = jnp.zeros_like(slab)

    def settle(which, k):
        def one(r, carry):
            rows = pl.ds(pl.multiple_of(r * 128, 128), 128)
            weight[rows, which * SLOT:which * SLOT + WID] = stage[which, rows, :]
            return carry

        lax.fori_loop(14 * k, 14 * k + 14, one, 0)

    def mask_z(dz):
        return pltpu.make_async_remote_copy(
            src_ref=masks.at[0, 0], dst_ref=masks.at[8 - dz, 0], send_sem=mz_sem.at[0, dz],
            recv_sem=mz_sem.at[1, 8 - dz], device_id=device(z=dz), device_id_type=MESH)

    def mask_y(dy):
        return pltpu.make_async_remote_copy(
            src_ref=masks.at[:, 0], dst_ref=masks.at[:, 4 - dy], send_sem=my_sem.at[0, dy],
            recv_sem=my_sem.at[1, 4 - dy], device_id=device(y=dy), device_id_type=MESH)

    def mask_arrived_z(dz):
        return pltpu.make_async_remote_copy(
            src_ref=masks.at[0, 0], dst_ref=masks.at[dz, 0], send_sem=mz_sem.at[0, dz],
            recv_sem=mz_sem.at[1, dz], device_id=device(z=dz), device_id_type=MESH)

    def mask_arrived_y(dy):
        return pltpu.make_async_remote_copy(
            src_ref=masks.at[:, 0], dst_ref=masks.at[:, dy], send_sem=my_sem.at[0, dy],
            recv_sem=my_sem.at[1, dy], device_id=device(y=dy), device_id_type=MESH)

    def prep(name, k):
        if name == "limits":
            limits(k)
        elif name == "places":
            places()
        elif name == "own":
            if k == 0:
                own_w.wait()
            settle(0, k)
        elif name == "other":
            if k == 0:
                give_w.wait_recv()
            settle(1, k)
        elif k == 0:
            for dz in range(1, NZ):
                mask_z(dz).start()
        else:
            for dz in range(1, NZ):
                mask_arrived_z(dz).wait_recv()
            for dy in range(1, NY):
                mask_y(dy).start()

    def window(dz):
        rows = held.at[dz]

        def multiply(n, carry):
            at = pl.ds(pl.multiple_of(n * TILE, TILE), TILE)
            logits[:, at] = jnp.dot(rows[...].reshape(ROWS, D), weight[:, at],
                                    preferred_element_type=jnp.float32)
            return carry

        lax.fori_loop(0, COLS // TILE, multiply, 0)
        source_z = lax.rem(z + dz, NZ)

        def group(dy, carry):
            source_y = lax.rem(y + dy, NY)
            first_row = (source_z * NY + source_y) * TOK + c * HALF
            limit = lim_col[pl.ds(pl.multiple_of(first_row, RB), HALF), :]
            peak = jnp.full((HALF, 128), NEG, jnp.float32)
            kept = []
            for j in range(COLS // 128):
                part = logits[pl.ds(pl.multiple_of(dy * HALF, RB), HALF), j * 128:(j + 1) * 128]
                part = jnp.where(cols[:, j * 128:(j + 1) * 128] < limit, part, NEG)
                kept.append(part)
                peak = jnp.maximum(peak, part)
            peak = jnp.max(peak, axis=1, keepdims=True)
            total = jnp.zeros((HALF, 128), jnp.float32)
            moment = jnp.zeros((HALF, 128), jnp.float32)
            for part in kept:
                shifted = part - peak
                e = jnp.exp(shifted)
                total = total + e
                moment = moment + e * shifted
            total = jnp.sum(total, axis=1, keepdims=True)
            moment = jnp.sum(moment, axis=1, keepdims=True)
            lane = lanes[:HALF]
            slab[pl.ds(pl.multiple_of(source_y * 64, 64), HALF), :] = jnp.where(
                lane == 0, peak, jnp.where(lane == 1, total, moment))
            return carry

        lax.fori_loop(0, NY, group, 0)
        across = slab[...].T
        for k in range(3):
            stat[dz, k] = across[k:k + 1]
        if dz:
            stat_copy(dz).start()

    def stat_copy(dz):
        return pltpu.make_async_remote_copy(
            src_ref=stat.at[dz], dst_ref=from_z.at[8 - dz], send_sem=rz_sem.at[0, dz],
            recv_sem=rz_sem.at[1, 8 - dz], device_id=device(z=dz), device_id_type=MESH)

    masks[0, 0] = jnp.zeros((1, 128), jnp.float32)
    masks[0, 0, :, 0:TOK] = mask_ref[...].astype(jnp.float32)
    first_send = True
    for step in STEPS:
        if step[0] == "send":
            _, axis, m, q = step
            started[q] = transfer(q, axis, m)
            started[q].start()
        else:
            if first_send:
                give_w.start()
                first_send = False
            if step[0] == "wait":
                started[step[1]].wait_recv()
            elif step[0] == "prep":
                prep(*step[1])
            else:
                window(step[1])

    for dz in range(1, NZ):
        pltpu.make_async_remote_copy(
            src_ref=stat.at[dz], dst_ref=from_z.at[dz], send_sem=rz_sem.at[0, dz],
            recv_sem=rz_sem.at[1, dz], device_id=device(z=dz), device_id_type=MESH).wait_recv()
    parts = [tuple(stat[0, k] for k in range(3))]
    parts += [tuple(from_z[dz, k] for k in range(3)) for dz in range(1, NZ)]
    merged = merge(parts)
    for k in range(3):
        plane[k] = merged[k]

    spots = [(dy, dx) for dy in range(NY) for dx in range(NX) if dy or dx]

    def plane_copy(dy, dx, arrive):
        back = (NY - dy) % NY * NX + (NX - dx) % NX
        slot = dy * NX + dx if arrive else back
        return pltpu.make_async_remote_copy(
            src_ref=plane, dst_ref=from_plane.at[slot], send_sem=rp_sem.at[0, dy * NX + dx],
            recv_sem=rp_sem.at[1, slot], device_id=device(y=dy, x=dx), device_id_type=MESH)

    for dy, dx in spots:
        plane_copy(dy, dx, False).start()
    for dy in range(1, NY):
        mask_arrived_y(dy).wait_recv()
    for dy, dx in spots:
        plane_copy(dy, dx, True).wait_recv()
    parts = [merged] + [tuple(from_plane[dy * NX + dx, k] for k in range(3)) for dy, dx in spots]
    peak, total, moment = merge(parts)
    entropy = jnp.log(total) - moment / total

    masked = jnp.zeros((1, 128), jnp.float32)
    found = []
    for k in range(2):
        owner = jnp.where(c == 0, 2 * z + k, 31 - 2 * z - k)
        column = jnp.broadcast_to(entropy[:, k * 128:(k + 1) * 128], (128, 128)).T
        spot = (owner * TOK).astype(jnp.float32) + lanes[:HALF].astype(jnp.float32)
        here_e = jnp.zeros((HALF, 128), jnp.float32)
        for h in range(2):
            source = pl.multiple_of((2 * k + h) * TOK + c * HALF, RB)
            here_e = here_e + jnp.where(pos_col[pl.ds(source, HALF), :] == spot,
                                        column[h * 64:h * 64 + HALF], 0.0)
        here_e = jnp.sum(here_e, axis=0, keepdims=True)
        found.append(here_e)
        dz = lax.rem(owner // NY - z + NZ, NZ)
        dy = lax.rem(lax.rem(owner, NY) - y + NY, NY)
        masked = masked + here_e * masks[dz, dy]
    masked = jnp.sum(masked, axis=1, keepdims=True)
    lane = lanes[:1]
    for k in range(2):
        ents[0, 0, k] = jnp.where(lane < TOK, found[k], masked if k == 0 else 0.0)

    others = [(dz, other) for dz in range(NZ) for other in range(2) if dz or other]

    def ent_copy(dz, other, arrive):
        slot = dz if arrive else (NZ - dz) % NZ
        target = device(z=dz, c=1) if other else device(z=dz)
        return pltpu.make_async_remote_copy(
            src_ref=ents.at[0, 0], dst_ref=ents.at[slot, other], send_sem=re_sem.at[0, dz, other],
            recv_sem=re_sem.at[1, slot, other], device_id=target, device_id_type=MESH)

    for dz, other in others:
        ent_copy(dz, other, False).start()

    started_count = jnp.sum(jnp.sum(masks[...].reshape(NZ * NY, 128), axis=0, keepdims=True), axis=1, keepdims=True)
    for k in range(len(TRANSFERS)):
        started[TRANSFERS[k]].wait_send()
    swap.wait_send()
    give_w.wait_send()
    for dz in range(1, NZ):
        mask_z(dz).wait_send()
        stat_copy(dz).wait_send()
    for dy in range(1, NY):
        mask_y(dy).wait_send()
    for dy, dx in spots:
        plane_copy(dy, dx, False).wait_send()

    for dz, other in others:
        ent_copy(dz, other, True).wait_recv()
    total_masked = jnp.zeros((1, 1), jnp.float32)
    for dz in range(NZ):
        for other in range(2):
            total_masked = total_masked + ents[dz, other, 0][:, TOK:TOK + 1]
    mean = total_masked / jnp.maximum(started_count, 1.0)
    mean_ref[...] = jnp.broadcast_to(mean, (1, 128))
    mine_s = z * NY + y
    index = jnp.where(z < NZ // 2, mine_s, 31 - mine_s)
    dz = lax.rem(index // 2 - z + NZ, NZ)
    other = jnp.where(z < NZ // 2, c, 1 - c)
    ent_ref[...] = ents[dz, other, lax.rem(index, 2)]
    for dz, other in others:
        ent_copy(dz, other, False).wait_send()


def local(hidden, lm_head, positions, vocab_limits, loss_mask):
    f32, bf16 = jnp.float32, jnp.bfloat16
    dma = pltpu.SemaphoreType.DMA
    any_space = pl.BlockSpec(memory_space=pl.ANY)
    vmem = pl.BlockSpec(memory_space=pltpu.VMEM)
    count = len(TRANSFERS)
    ent, mean = pl.pallas_call(
        kernel,
        out_shape=(jax.ShapeDtypeStruct((1, 128), f32), jax.ShapeDtypeStruct((1, 128), f32)),
        in_specs=[any_space, any_space, vmem, vmem, vmem],
        out_specs=(vmem, vmem),
        scratch_shapes=[
            pltpu.VMEM((NZ, NY, COLORS, RB, D), bf16),
            pltpu.VMEM((D, COLS), bf16),
            pltpu.VMEM((2, D, WID), bf16),
            pltpu.VMEM((TOK, FEAT // 2), bf16),
            pltpu.VMEM((HALF, FEAT // 2), bf16),
            pltpu.VMEM((ROWS, COLS), f32),
            pltpu.VMEM((2, 128, 128), f32),
            pltpu.VMEM((NZ * NY * TOK, 128), f32),
            pltpu.VMEM((3 * 128, 128), f32),
            pltpu.VMEM((1, COLS), f32),
            pltpu.VMEM((256, 128), f32),
            pltpu.VMEM((NZ, 3, 1, 256), f32),
            pltpu.VMEM((NZ, 3, 1, 256), f32),
            pltpu.VMEM((3, 1, 256), f32),
            pltpu.VMEM((NY * NX, 3, 1, 256), f32),
            pltpu.VMEM((NZ, 2, 2, 1, 128), f32),
            pltpu.VMEM((NZ, NY, 1, 128), f32),
            dma((count,)), dma((count,)), dma((2,)), dma((2,)),
            dma((2, NZ)), dma((2, NY)), dma((2, NZ)), dma((2, NY * NX)), dma((2, NZ, 2)), dma((2,)),
        ],
        compiler_params=pltpu.CompilerParams(
            collective_id=0, has_side_effects=True, vmem_limit_bytes=62 * 2**20),
    )(hidden, lm_head, positions.reshape(24, 128), vocab_limits.reshape(24, 128), loss_mask.reshape(1, TOK))
    return ent[0, :TOK], mean[0, 0]


def solution(mesh):
    torus = Mesh(mesh.devices.reshape(NZ, NY, NX, 2), AXES)
    in_specs = (P(("z", "y"), ("x", "c")), P(None, AXES), P(), P(), P(("z", "y")))
    return jax.shard_map(local, mesh=torus, in_specs=in_specs, out_specs=(P(("z", "y")), P()), check_vma=False)
```

time: 299 us -> 96.4 us (0.32)
  waiting for transfers between devices: 158 us -> 0 us
  Pallas kernels: 0 us -> 85.4 us
  blocking collectives: 81.8 us -> 0 us
  matrix products: 18.4 us -> 0 us
  between operations: 16.7 us -> 2.39 us
  local copies, waits for them, and re-layouts: 17.1 us -> 8.29 us
  other arithmetic: 6.95 us -> 0 us
    all_gather x2 -> x0, waiting for transfers between devices: 158 us -> none  [the longest x1 109 us: local(): lax.all_gather(all_tokens, VOCAB, axis=1, tiled=True)]
    pallas_call x0 -> x1, Pallas kernels: none -> 85.4 us  [local(): pl.pallas_call(kernel, out_shape=(jax.ShapeDtypeStruct((1, 128), f32), ja...]
    all_gather x5 -> x0, blocking collectives: 66 us -> none  [the longest x4 53 us: gathered_once(): both, at, found = (lax.all_gather(jnp.concatenate(lines), axis), 0, {})]
    dot_general x1 -> x0, matrix products: 18.4 us -> none  [local(): jnp.dot(lax.all_gather(all_tokens, VOCAB, axis=1, tiled=True), lm_head, p...]
    all_to_all x1 -> x0, blocking collectives: 15.9 us -> none  [copy_for_each(): return lax.all_to_all(copies, axis, split_axis=0, concat_axis=0, tiled=True)]
    scatter x1 -> x0, local copies, waits for them, and re-layouts: 11.8 us -> none  [local(): jnp.zeros((tokens_all,), jnp.float32).at[positions].set(entropy_rows)]
    unnamed x6 -> x1, local copies, waits for them, and re-layouts: 0.01 us -> 7.12 us
    all_gather x1 -> x0, local copies, waits for them, and re-layouts: 4.63 us -> none  [gather_axes(): whole = lax.all_gather(whole, axes[number], axis=dim, tiled=True)]
  transfers between devices with their start and end apart: 2 -> 0, of which waited for: 2 -> 0; matrix products, arithmetic and copies ran while one was open for 0% -> 0% of each run, Pallas kernels for 0% -> 0%
where the time goes in v1:
time: 96.4 us; the launch traced here: 96.1 us
  Pallas kernels  85.4 us (89%)
  local copies, waits for them, and re-layouts  8.29 us (9%)
  between operations  2.39 us (2%)
    pallas_call x1, Pallas kernels, local(): pl.pallas_call(kernel, out_shape=(jax.ShapeDtypeStruct((1, 128), f32), ja...  85.4 us
    unnamed x1, local copies, waits for them, and re-layouts  7.12 us

profile of v1, /device:TPU:1, one launch (start us, length us, event | category | flops | bytes accessed | tf_op | source)
XLA Modules:
  0.0 96.1 jit_solution(10568701826216579608)
XLA Ops:
  0.6 7.1 %copy.7.lm_ref = bf16[3584,594]{1,0:T(8,128)(2,1)} copy(bf16[3584,594]{0,1:T(8,128)(2,1)} %param.6) | data formatting | bytes 8515584 | tf_op args[1]
  7.7 85.4 %shard_map.68 = (f32[1,128]{1,0:T(1,128)}, f32[1,128]{1,0:T(1,128)}) custom-call(bf16[96,448]{1,0:T(8,128)(2,1)} %hid_ref.1, bf16[3584,594]{1,0:T(8,128)(2,1)} %copy.7.lm_ref, s32[24,128]{1,0:T(8,128)} %bitcast.7, s32[24,128]{1,0:T(8,128)} %bitcast.8, s32[1,96]{1,0:T(1,128)} %bitcast.9), custom_call_target="tpu_custom_call" | custom-call | tf_op jit(solution)/shard_map/pallas_call | solution.py:535
  93.1 1.2 %slice_bitcast_fusion = f32[96]{0:T(128)} fusion(f32[1,128]{1,0:T(1,128)} %get-tuple-element.4), kind=kLoop, calls=%fused_computation | loop fusion | bytes 768 | tf_op jit(solution)/shard_map/squeeze | solution.py:564

commit v2 on v1

--- a/solution.py
+++ b/solution.py
@@ -14,16 +14,15 @@
 MESH = pl.DeviceIdType.MESH
 HALF, RB, COLORS = 48, 16, 3
 TOK = 96
-ROWS = NY * HALF
 D, FEAT = 3584, 896
-WID, SLOT = 594, 640
-COLS = 2 * SLOT
-TILE = 256
+WID, PAD = 594, 608
+GROUP = 64
+LANES = NY * GROUP
 NEG = -1e30
-ORDER = (0, 1, 7, 2, 6, 3, 5, 4)
-DEADLINE = (8.7, 7.5, 14.8, 17.9, 19.6)
-UNIT, HOP, BACKLOG = 0.615, 1.75, 2.0
-WINDOW = 2.9
+ORDER = (1, 7, 2, 6, 3, 5, 4, 0)
+DEADLINE = (17.7, 10.3, 11.8, 14.5, 16.9, 16.7, 12.6, 10.1)
+UNIT, HOP, BACKLOG = 0.615, 1.75, 1.5
+WINDOW = 2.6
 
 
 def onward(n, d, far):
@@ -102,7 +101,7 @@
     def latest(p):
         if p not in due:
             dz = window_of(p)
-            k = DEADLINE[min(dz, 8 - dz)]
+            k = DEADLINE[dz]
             ahead = sends_of(p)
             launch = launch_of(p)
             if launch:
@@ -142,12 +141,15 @@
             have.add(launch)
             offer(sends_of(launch))
 
+    def blocked():
+        return any(p[0][0] == "other" for p in preps)
+
     for p in (("A", "y", 0), ("B", "z", 0), ("C", "z", 0)):
         take(p)
     pump()
     left = list(ORDER)
     preps = list(preps)
-    while flying or left:
+    while flying or left or preps:
         if flying and flying[0][0] <= now:
             _, _, q = heapq.heappop(flying)
             steps.append(("wait", q))
@@ -161,10 +163,12 @@
             now += cost
             pump()
             continue
-        ready = [] if preps else [w for w in left if all(q in have for q in pieces_of_window(w))]
+        ready = [] if blocked() else [w for w in left if all(q in have for q in pieces_of_window(w))]
+        if len(left) > 1:
+            ready = [w for w in ready if w]
         if ready:
+            steps.append(("window", ready[0]))
             left.remove(ready[0])
-            steps.append(("window", ready[0]))
             now += WINDOW
             pump()
             continue
@@ -172,17 +176,16 @@
         if preps:
             nxt.append(preps[0][1])
         now = max(now, min(nxt))
-    return steps
+    return steps, now
 
 
 PREPS = (
-    [(("limits", k), 0.2, 0.45) for k in range(6)]
-    + [(("places", 0), 3.0, 0.4)]
-    + [(("own", k), 4.0, 0.3) for k in range(2)]
+    [(("limits", 0), 0.2, 0.3), (("places", 0), 0.8, 0.4)]
+    + [(("own", k), 3.0, 0.3) for k in range(2)]
     + [(("other", k), 11.0, 0.3) for k in range(2)]
-    + [(("mask", 0), 12.0, 0.1), (("mask", 1), 17.0, 0.1)]
+    + [(("mask", 0), 16.0, 0.1), (("mask", 1), 32.0, 0.1)]
 )
-STEPS = plan(PREPS)
+STEPS, _ = plan(PREPS)
 TRANSFERS = [s[3] for s in STEPS if s[0] == "send"]
 NUMBER = {q: k for k, q in enumerate(TRANSFERS)}
 
@@ -202,8 +205,8 @@
 
 
 def kernel(hid_ref, lm_ref, pos_ref, lim_ref, mask_ref, ent_ref, mean_ref,
-           held, weight, stage, hstage, pstage, logits, turned, lim_col, pos_col, cols,
-           slab, stat, from_z, plane, from_plane, ents, masks,
+           held, weight, stage, hstage, pstage, logits, small, mask_in, lim_row, pos_col,
+           stat, from_z, plane, from_plane, ents, masks,
            send_sem, recv_sem, hx_sem, w_sem, mz_sem, my_sem, rz_sem, rp_sem, re_sem, copy_sem):
     z, y, x, c = (lax.axis_index(a) for a in AXES)
     here = {"z": z, "y": y, "x": x, "c": c}
@@ -216,14 +219,21 @@
     own_h = pltpu.make_async_copy(hid_ref, hstage, copy_sem.at[1])
     own_h.start()
     own_w.start()
+    given = [pltpu.make_async_copy(lim_ref, small.at[0], copy_sem.at[2]),
+             pltpu.make_async_copy(pos_ref, small.at[1], copy_sem.at[3]),
+             pltpu.make_async_copy(mask_ref, mask_in, copy_sem.at[4])]
+    for copy in given:
+        copy.start()
 
     barrier = pltpu.get_barrier_semaphore()
     near = [device(**{a: d}) for a in "zyx" for d in (1, SIZE[a] - 1)] + [device(c=1)]
     for who in near:
         pl.semaphore_signal(barrier, inc=1, device_id=who, device_id_type=MESH)
-    pl.semaphore_wait(barrier, len(near))
-
-    own_h.wait()
+    with jax.named_scope("T_barrier"):
+        pl.semaphore_wait(barrier, len(near))
+
+    with jax.named_scope("T_ownh"):
+        own_h.wait()
     swap = pltpu.make_async_remote_copy(
         src_ref=hstage.at[pl.ds(pl.multiple_of((1 - c) * HALF, RB), HALF), :], dst_ref=pstage,
         send_sem=hx_sem.at[0], recv_sem=hx_sem.at[1], device_id=device(c=1), device_id_type=MESH)
@@ -236,30 +246,34 @@
         return pl.ds(pl.multiple_of(lax.rem(x + dx, NX) * FEAT, 128), FEAT)
 
     mine = hstage[pl.ds(pl.multiple_of(c * HALF, RB), HALF), :].astype(jnp.float32)
-    swap.wait_recv()
+    with jax.named_scope("T_swap"):
+        swap.wait_recv()
     theirs = pstage[...].astype(jnp.float32)
     first = c == 0
     left = jnp.where(first, mine, theirs)
     right = jnp.where(first, theirs, mine)
     both = jnp.concatenate([left, right], axis=1).astype(jnp.bfloat16)
     for k in range(COLORS):
-        held[0, 0, k, :, feature(0)] = both[k * RB:(k + 1) * RB]
+        held[0, 0, k * RB:(k + 1) * RB, feature(0)] = both[k * RB:(k + 1) * RB]
+
+    def block(k):
+        return pl.ds(k * RB, RB)
 
     def place(p):
         color, axis = p[0], p[1]
         if color == "A":
             if axis == "z":
-                return held.at[p[2], p[3], 0]
-            return held.at[0, p[2], 0, :, feature(0 if axis == "y" else p[3])]
+                return held.at[p[2], p[3], block(0)]
+            return held.at[0, p[2], block(0), feature(0 if axis == "y" else p[3])]
         if axis == "z":
-            return held.at[p[2], 0, 1 if color == "B" else 2, :, feature(0)]
+            return held.at[p[2], 0, block(1 if color == "B" else 2), feature(0)]
         if color == "B":
             if axis == "y":
-                return held.at[p[2], p[3], 1, :, feature(0)]
-            return held.at[p[2], :, 1, :, feature(p[3])]
+                return held.at[p[2], p[3], block(1), feature(0)]
+            return held.at[p[2], :, block(1), feature(p[3])]
         if axis == "x":
-            return held.at[p[2], 0, 2, :, feature(p[3])]
-        return held.at[p[2], p[3], 2]
+            return held.at[p[2], 0, block(2), feature(p[3])]
+        return held.at[p[2], p[3], block(2)]
 
     def transfer(q, axis, m):
         k = NUMBER[q]
@@ -276,11 +290,11 @@
             src = dst_at = None
             column = feature(q[-1] + m + NX)
             if q[0] == "A":
-                src = dst_at = held.at[0, q[2], 0, :, column]
+                src = dst_at = held.at[0, q[2], block(0), column]
             elif q[0] == "B":
-                src = dst_at = held.at[q[2], :, 1, :, column]
+                src = dst_at = held.at[q[2], :, block(1), column]
             else:
-                src = dst_at = held.at[q[2], 0, 2, :, column]
+                src = dst_at = held.at[q[2], 0, block(2), column]
             dst = dst_at
         else:
             src = place(source)
@@ -291,37 +305,38 @@
     started = {}
     lanes = lax.broadcasted_iota(jnp.int32, (128, 128), 1)
 
-    def limits(k):
-        if k == 0:
-            pad = jnp.zeros((128 - 24, 128), jnp.float32)
-            turned[0] = jnp.concatenate([lim_ref[...].astype(jnp.float32), pad], axis=0).T
-            turned[1] = jnp.concatenate([pos_ref[...].astype(jnp.float32), pad], axis=0).T
-            j = lax.broadcasted_iota(jnp.int32, (1, COLS), 1)
-            number = (z * NY + y) * (2 * NX) + x * 2
-            start = jnp.where(j < SLOT, (number + c) * WID, (number + 1 - c) * WID - SLOT)
-            inside = jnp.where(j < SLOT, j, j - SLOT) < WID
-            cols[...] = jnp.where(inside, start + j, 1 << 28).astype(jnp.float32)
-
-        def one(r, carry):
-            column = jnp.sum(jnp.where(lanes == r, turned[0], 0.0), axis=1, keepdims=True)
-            lim_col[pl.ds(pl.multiple_of(r * 128, 128), 128), :] = jnp.broadcast_to(column, (128, 128))
-            return carry
-
-        lax.fori_loop(4 * k, 4 * k + 4, one, 0)
+    def limits():
+        for copy in given:
+            copy.wait()
+        masks[0, 0] = jnp.zeros((1, 128), jnp.float32)
+        masks[0, 0, :, 0:TOK] = mask_in[...].astype(jnp.float32)
+        table = jnp.concatenate([small[0, pl.ds(j, NZ, stride=3), :] for j in range(3)], axis=1)
+        row = lax.broadcasted_iota(jnp.int32, (3 * 128, LANES), 0)
+        column = lax.broadcasted_iota(jnp.int32, (3 * 128, LANES), 1)
+        dy, i = column // GROUP, column % GROUP
+        want = lax.rem(y + dy, NY) * TOK + c * HALF + i
+        pick = jnp.where((row == want) & (i < HALF), 1.0, 0.0).astype(jnp.bfloat16)
+        found = jnp.zeros((NZ, LANES), jnp.float32)
+        for shift in (14, 7, 0):
+            digit = lax.bitwise_and(lax.shift_right_logical(table, shift), 127)
+            digit = digit.astype(jnp.float32).astype(jnp.bfloat16)
+            found = found * 128.0 + jnp.dot(digit, pick, preferred_element_type=jnp.float32)
+        lim_row[...] = found.astype(jnp.int32)
 
     def places():
+        pad = jnp.zeros((128 - 24, 128), jnp.float32)
+        turned = jnp.concatenate([small[1].astype(jnp.float32), pad], axis=0).T
         for k in range(3):
-            column = jnp.sum(jnp.where(lanes == 3 * z + k, turned[1], 0.0), axis=1, keepdims=True)
+            column = jnp.sum(jnp.where(lanes == 3 * z + k, turned, 0.0), axis=1, keepdims=True)
             pos_col[k * 128:(k + 1) * 128, :] = jnp.broadcast_to(column, (128, 128))
-        slab[...] = jnp.zeros_like(slab)
 
     def settle(which, k):
         def one(r, carry):
-            rows = pl.ds(pl.multiple_of(r * 128, 128), 128)
-            weight[rows, which * SLOT:which * SLOT + WID] = stage[which, rows, :]
+            at = pl.ds(pl.multiple_of(r * 256, 128), 256)
+            weight[which, 0:WID, at] = stage[which, :, at]
             return carry
 
-        lax.fori_loop(14 * k, 14 * k + 14, one, 0)
+        lax.fori_loop(7 * k, 7 * k + 7, one, 0)
 
     def mask_z(dz):
         return pltpu.make_async_remote_copy(
@@ -345,7 +360,7 @@
 
     def prep(name, k):
         if name == "limits":
-            limits(k)
+            limits()
         elif name == "places":
             places()
         elif name == "own":
@@ -365,48 +380,34 @@
             for dy in range(1, NY):
                 mask_y(dy).start()
 
-    def window(dz):
-        rows = held.at[dz]
-
-        def multiply(n, carry):
-            at = pl.ds(pl.multiple_of(n * TILE, TILE), TILE)
-            logits[:, at] = jnp.dot(rows[...].reshape(ROWS, D), weight[:, at],
-                                    preferred_element_type=jnp.float32)
-            return carry
-
-        lax.fori_loop(0, COLS // TILE, multiply, 0)
-        source_z = lax.rem(z + dz, NZ)
-
-        def group(dy, carry):
-            source_y = lax.rem(y + dy, NY)
-            first_row = (source_z * NY + source_y) * TOK + c * HALF
-            limit = lim_col[pl.ds(pl.multiple_of(first_row, RB), HALF), :]
-            peak = jnp.full((HALF, 128), NEG, jnp.float32)
-            kept = []
-            for j in range(COLS // 128):
-                part = logits[pl.ds(pl.multiple_of(dy * HALF, RB), HALF), j * 128:(j + 1) * 128]
-                part = jnp.where(cols[:, j * 128:(j + 1) * 128] < limit, part, NEG)
-                kept.append(part)
-                peak = jnp.maximum(peak, part)
-            peak = jnp.max(peak, axis=1, keepdims=True)
-            total = jnp.zeros((HALF, 128), jnp.float32)
-            moment = jnp.zeros((HALF, 128), jnp.float32)
-            for part in kept:
-                shifted = part - peak
-                e = jnp.exp(shifted)
-                total = total + e
-                moment = moment + e * shifted
-            total = jnp.sum(total, axis=1, keepdims=True)
-            moment = jnp.sum(moment, axis=1, keepdims=True)
-            lane = lanes[:HALF]
-            slab[pl.ds(pl.multiple_of(source_y * 64, 64), HALF), :] = jnp.where(
-                lane == 0, peak, jnp.where(lane == 1, total, moment))
-            return carry
-
-        lax.fori_loop(0, NY, group, 0)
-        across = slab[...].T
+    number = (z * NY + y) * (2 * NX) + x * 2
+    starts = ((number + c) * WID, (number + 1 - c) * WID)
+    depth = lax.broadcasted_iota(jnp.int32, (PAD, LANES), 0)
+
+    def multiply(dz, slot):
+        for k in range(2):
+            logits[slot, k] = lax.dot_general(
+                weight[k], held[dz].reshape(LANES, D), (((1,), (1,)), ((), ())),
+                preferred_element_type=jnp.float32)
+
+    def reduce_rows(dz, slot):
+        limit = lim_row[pl.ds(lax.rem(z + dz, NZ), 1), :]
+        peak = jnp.full((1, LANES), NEG, jnp.float32)
+        for k in range(2):
+            bound = jnp.minimum(limit - starts[k], WID)
+            logits[slot, k] = jnp.where(depth < bound, logits[slot, k], NEG)
+            peak = jnp.maximum(peak, jnp.max(logits[slot, k], axis=0, keepdims=True))
+        total = jnp.zeros((1, LANES), jnp.float32)
+        moment = jnp.zeros((1, LANES), jnp.float32)
+        for k in range(2):
+            shifted = logits[slot, k] - peak
+            e = jnp.exp(shifted)
+            total = total + jnp.sum(e, axis=0, keepdims=True)
+            moment = moment + jnp.sum(e * shifted, axis=0, keepdims=True)
+        rows = jnp.concatenate([peak, total, moment, jnp.zeros((5, LANES), jnp.float32)], axis=0)
+        rows = pltpu.roll(rows, y * GROUP, 1)
         for k in range(3):
-            stat[dz, k] = across[k:k + 1]
+            stat[dz, k] = rows[k:k + 1]
         if dz:
             stat_copy(dz).start()
 
@@ -415,8 +416,16 @@
             src_ref=stat.at[dz], dst_ref=from_z.at[8 - dz], send_sem=rz_sem.at[0, dz],
             recv_sem=rz_sem.at[1, 8 - dz], device_id=device(z=dz), device_id_type=MESH)
 
-    masks[0, 0] = jnp.zeros((1, 128), jnp.float32)
-    masks[0, 0, :, 0:TOK] = mask_ref[...].astype(jnp.float32)
+    done = []
+
+    def window(dz):
+        if done:
+            reduce_rows(done[-1], len(done) % 2)
+        if dz is None:
+            return
+        done.append(dz)
+        multiply(dz, len(done) % 2)
+
     first_send = True
     for step in STEPS:
         if step[0] == "send":
@@ -433,11 +442,14 @@
                 prep(*step[1])
             else:
                 window(step[1])
-
-    for dz in range(1, NZ):
-        pltpu.make_async_remote_copy(
-            src_ref=stat.at[dz], dst_ref=from_z.at[dz], send_sem=rz_sem.at[0, dz],
-            recv_sem=rz_sem.at[1, dz], device_id=device(z=dz), device_id_type=MESH).wait_recv()
+    with jax.named_scope("T_last"):
+        window(None)
+
+    with jax.named_scope("T_zround"):
+        for dz in range(1, NZ):
+            pltpu.make_async_remote_copy(
+                src_ref=stat.at[dz], dst_ref=from_z.at[dz], send_sem=rz_sem.at[0, dz],
+                recv_sem=rz_sem.at[1, dz], device_id=device(z=dz), device_id_type=MESH).wait_recv()
     parts = [tuple(stat[0, k] for k in range(3))]
     parts += [tuple(from_z[dz, k] for k in range(3)) for dz in range(1, NZ)]
     merged = merge(parts)
@@ -457,8 +469,9 @@
         plane_copy(dy, dx, False).start()
     for dy in range(1, NY):
         mask_arrived_y(dy).wait_recv()
-    for dy, dx in spots:
-        plane_copy(dy, dx, True).wait_recv()
+    with jax.named_scope("T_planeround"):
+        for dy, dx in spots:
+            plane_copy(dy, dx, True).wait_recv()
     parts = [merged] + [tuple(from_plane[dy * NX + dx, k] for k in range(3)) for dy, dx in spots]
     peak, total, moment = merge(parts)
     entropy = jnp.log(total) - moment / total
@@ -509,19 +522,18 @@
     for dy, dx in spots:
         plane_copy(dy, dx, False).wait_send()
 
-    for dz, other in others:
-        ent_copy(dz, other, True).wait_recv()
-    total_masked = jnp.zeros((1, 1), jnp.float32)
-    for dz in range(NZ):
-        for other in range(2):
-            total_masked = total_masked + ents[dz, other, 0][:, TOK:TOK + 1]
+    with jax.named_scope("T_entround"):
+        for dz, other in others:
+            ent_copy(dz, other, True).wait_recv()
+    total_masked = jnp.sum(ents[:, :, 0].reshape(2 * NZ, 128), axis=0, keepdims=True)
+    total_masked = jnp.sum(jnp.where(lane == TOK, total_masked, 0.0), axis=1, keepdims=True)
     mean = total_masked / jnp.maximum(started_count, 1.0)
     mean_ref[...] = jnp.broadcast_to(mean, (1, 128))
     mine_s = z * NY + y
     index = jnp.where(z < NZ // 2, mine_s, 31 - mine_s)
     dz = lax.rem(index // 2 - z + NZ, NZ)
     other = jnp.where(z < NZ // 2, c, 1 - c)
-    ent_ref[...] = ents[dz, other, lax.rem(index, 2)]
+    ent_ref[...] = ents[dz, other, lax.rem(index, 2)][:, 0:TOK]
     for dz, other in others:
         ent_copy(dz, other, False).wait_send()
 
@@ -534,21 +546,20 @@
     count = len(TRANSFERS)
     ent, mean = pl.pallas_call(
         kernel,
-        out_shape=(jax.ShapeDtypeStruct((1, 128), f32), jax.ShapeDtypeStruct((1, 128), f32)),
-        in_specs=[any_space, any_space, vmem, vmem, vmem],
+        out_shape=(jax.ShapeDtypeStruct((1, TOK), f32), jax.ShapeDtypeStruct((1, 128), f32)),
+        in_specs=[any_space] * 5,
         out_specs=(vmem, vmem),
         scratch_shapes=[
-            pltpu.VMEM((NZ, NY, COLORS, RB, D), bf16),
-            pltpu.VMEM((D, COLS), bf16),
-            pltpu.VMEM((2, D, WID), bf16),
+            pltpu.VMEM((NZ, NY, GROUP, D), bf16),
+            pltpu.VMEM((2, PAD, D), bf16),
+            pltpu.VMEM((2, WID, D), bf16),
             pltpu.VMEM((TOK, FEAT // 2), bf16),
             pltpu.VMEM((HALF, FEAT // 2), bf16),
-            pltpu.VMEM((ROWS, COLS), f32),
-            pltpu.VMEM((2, 128, 128), f32),
-            pltpu.VMEM((NZ * NY * TOK, 128), f32),
+            pltpu.VMEM((2, 2, PAD, LANES), f32),
+            pltpu.VMEM((2, 24, 128), jnp.int32),
+            pltpu.VMEM((1, TOK), jnp.int32),
+            pltpu.VMEM((NZ, LANES), jnp.int32),
             pltpu.VMEM((3 * 128, 128), f32),
-            pltpu.VMEM((1, COLS), f32),
-            pltpu.VMEM((256, 128), f32),
             pltpu.VMEM((NZ, 3, 1, 256), f32),
             pltpu.VMEM((NZ, 3, 1, 256), f32),
             pltpu.VMEM((3, 1, 256), f32),
@@ -556,12 +567,12 @@
             pltpu.VMEM((NZ, 2, 2, 1, 128), f32),
             pltpu.VMEM((NZ, NY, 1, 128), f32),
             dma((count,)), dma((count,)), dma((2,)), dma((2,)),
-            dma((2, NZ)), dma((2, NY)), dma((2, NZ)), dma((2, NY * NX)), dma((2, NZ, 2)), dma((2,)),
+            dma((2, NZ)), dma((2, NY)), dma((2, NZ)), dma((2, NY * NX)), dma((2, NZ, 2)), dma((5,)),
         ],
         compiler_params=pltpu.CompilerParams(
             collective_id=0, has_side_effects=True, vmem_limit_bytes=62 * 2**20),
-    )(hidden, lm_head, positions.reshape(24, 128), vocab_limits.reshape(24, 128), loss_mask.reshape(1, TOK))
-    return ent[0, :TOK], mean[0, 0]
+    )(hidden, lm_head.T, positions.reshape(24, 128), vocab_limits.reshape(24, 128), loss_mask.reshape(1, TOK))
+    return ent.reshape(TOK), mean[0, 0]
 
 
 def solution(mesh):

time: 96.4 us -> 85.5 us (0.89)
  local copies, waits for them, and re-layouts: 8.29 us -> 1.11 us
  Pallas kernels: 85.4 us -> 81.9 us
    unnamed x1, local copies, waits for them, and re-layouts: 7.12 us -> 1.11 us
    pallas_call x1, Pallas kernels: 85.4 us -> 81.9 us  [local(): pl.pallas_call(kernel, out_shape=(jax.ShapeDtypeStruct((1, TOK), f32), ja...]
    squeeze x1 -> x0, local copies, waits for them, and re-layouts: 1.17 us -> none  [local(): return (ent[0, :TOK], mean[0, 0])]
where the time goes in v2:
time: 85.5 us; the launch traced here: 85.4 us
  Pallas kernels  81.9 us (96%)
  between operations  2.4 us (3%)
  local copies, waits for them, and re-layouts  1.11 us (1%)
    pallas_call x1, Pallas kernels, local(): pl.pallas_call(kernel, out_shape=(jax.ShapeDtypeStruct((1, TOK), f32), ja...  81.9 us

profile of v2, /device:TPU:1, one launch (start us, length us, event | category | flops | bytes accessed | tf_op | source)
XLA Modules:
  0.0 85.4 jit_solution(17567940529777402202)
XLA Ops:
  0.6 81.9 %shard_map.68 = (f32[1,96]{1,0:T(1,128)}, f32[1,128]{1,0:T(1,128)}) custom-call(bf16[96,448]{1,0:T(8,128)(2,1)} %hid_ref.1, bf16[594,3584]{1,0:T(8,128)(2,1)} %bitcast.7, s32[24,128]{1,0:T(8,128)} %bitcast.8, s32[24,128]{1,0:T(8,128)} %bitcast.9, s32[1,96]{1,0:T(1,128)} %bitcast.10), custom_call_target="tpu_custom_call" | custom-call | tf_op jit(solution)/shard_map/pallas_call | solution.py:547
  82.6 1.1 %copy.9 = f32[96]{0:T(128)} copy(f32[96]{0:T(128)} %bitcast.12) | data formatting | bytes 768

commit v3 on v2

v3 whole, which is shorter than its diff:
```python
import heapq

import jax
import jax.numpy as jnp
from jax import lax
from jax.experimental import pallas as pl
from jax.experimental.pallas import tpu as pltpu
from jax.sharding import Mesh
from jax.sharding import PartitionSpec as P

NZ, NY, NX = 8, 4, 4
SIZE = {"z": NZ, "y": NY, "x": NX}
AXES = ("z", "y", "x", "c")
MESH = pl.DeviceIdType.MESH
HALF, RB, COLORS = 48, 16, 3
TOK = 96
D, FEAT = 3584, 896
WID, PAD = 594, 608
CHUNK, LANES = 64, 256
WINDOWS = NZ * COLORS * CHUNK // LANES
NEG = -1e30
DEADLINE = (
    (18.1, 16.1, 16.7),
    (19.9, 17.9, 18.5),
    (23.9, 21.9, 22.5),
    (24.8, 22.8, 23.4),
    (26.9, 24.9, 25.5),
    (24.1, 22.1, 22.7),
    (24.2, 22.2, 22.8),
    (23.8, 21.8, 22.4),
)
UNIT, HOP, BACKLOG = 0.615, 1.75, 1.5
WINDOW = 3.05


def onward(n, d, far):
    if d == 0:
        return [1, -1]
    if d < n // 2:
        return [-1] if d + 1 < n // 2 or far == -1 else []
    if d > n // 2:
        return [1] if d - 1 > n // 2 or far == 1 else []
    return []


def parity(k):
    return 1 if k % 2 == 0 else -1


def sends_of(p):
    color, axis, rest = p[0], p[1], p[2:]
    out = []
    if color == "A" and axis == "y":
        (dy,) = rest
        out += [("y", m, 1, ("A", "y", (dy - m) % 4)) for m in onward(4, dy, 1)]
        out += [("x", m, 1, ("A", "x", dy, -m % 4)) for m in (1, -1)]
    elif color == "A" and axis == "x":
        dy, dx = rest
        out += [("x", m, 1, ("A", "x", dy, (dx - m) % 4)) for m in onward(4, dx, parity(dy))]
    elif color == "A":
        dz, dy = rest
        out += [("z", m, 4, ("A", "z", (dz - m) % 8, dy)) for m in onward(8, dz, parity(dy))]
    elif axis == "z":
        (dz,) = rest
        far = 1 if color == "B" else -1
        out += [("z", m, 1, (color, "z", (dz - m) % 8)) for m in onward(8, dz, far)]
        second = "y" if color == "B" else "x"
        out += [(second, m, 1, (color, second, dz, -m % 4)) for m in (1, -1)]
    else:
        dz, d = rest
        last = (color, axis) in (("B", "x"), ("C", "y"))
        size = 4 if last else 1
        out += [(axis, m, size, (color, axis, dz, (d - m) % 4)) for m in onward(4, d, parity(dz))]
    return out


def launch_of(p):
    color, axis = p[0], p[1]
    if color == "A" and axis != "z":
        return ("A", "z", 0, p[2])
    if color == "B" and axis != "x":
        return ("B", "x", p[2], 0)
    if color == "C" and axis != "y":
        return ("C", "y", p[2], 0)
    return None


def parts_of(launch):
    color, _, a, b = launch
    if color == "A":
        return [("A", "y", b)] + [("A", "x", b, k) for k in (1, 2, 3)]
    if color == "B":
        return [("B", "z", a)] + [("B", "y", a, k) for k in (1, 2, 3)]
    return [("C", "z", a)] + [("C", "x", a, k) for k in (1, 2, 3)]


def window_of(p):
    return 0 if p[0] == "A" and p[1] != "z" else p[2]


def pieces_of_chunk(dz, color):
    last = (("A", "z"), ("B", "x"), ("C", "y"))[color]
    return [(*last, dz, k) for k in range(4)]


def plan(preps, chunks=None):
    due = {}

    def latest(p):
        if p not in due:
            dz = window_of(p)
            k = DEADLINE[dz][{"A": 0, "B": 1, "C": 2}[p[0]]]
            ahead = sends_of(p)
            launch = launch_of(p)
            if launch:
                ahead = ahead + sends_of(launch)
            for _, _, size, q in ahead:
                k = min(k, latest(q) - HOP - size * UNIT - 0.3)
            due[p] = k
        return due[p]

    free = {(a, m): 0.0 for a in "xyz" for m in (1, -1)}
    waiting = {k: [] for k in free}
    have, steps, flying = set(), [], []
    count = 0
    now = 0.0

    def offer(sends):
        nonlocal count
        for axis, m, size, q in sends:
            heapq.heappush(waiting[axis, m], (latest(q) - size * UNIT, count, size, q))
            count += 1

    def pump():
        nonlocal count
        for link in free:
            while waiting[link] and free[link] - now < BACKLOG:
                _, _, size, q = heapq.heappop(waiting[link])
                free[link] = max(free[link], now) + size * UNIT
                heapq.heappush(flying, (free[link] + HOP, count, q))
                count += 1
                steps.append(("send", link[0], link[1], q))

    def take(p):
        have.add(p)
        offer(sends_of(p))
        launch = launch_of(p)
        if launch and launch not in have and all(q in have for q in parts_of(launch)):
            have.add(launch)
            offer(sends_of(launch))

    def blocked():
        return any(p[0][0] == "other" for p in preps)

    for p in (("A", "y", 0), ("B", "z", 0), ("C", "z", 0)):
        take(p)
    pump()
    arrived = {}
    left = list(range(WINDOWS)) if chunks else []
    preps = list(preps)
    while flying or left or preps:
        if flying and flying[0][0] <= now:
            _, _, q = heapq.heappop(flying)
            steps.append(("wait", q))
            arrived[q] = now
            take(q)
            pump()
            now += 0.03
            continue
        if preps and now >= preps[0][1]:
            name, _, cost = preps.pop(0)
            steps.append(("prep", name))
            now += cost
            pump()
            continue
        ready = [] if blocked() else [w for w in left if all(
            q in have for chunk in chunks[4 * w:4 * w + 4] for q in pieces_of_chunk(*chunk))]
        if ready:
            steps.append(("window", ready[0]))
            left.remove(ready[0])
            now += WINDOW
            pump()
            continue
        nxt = [flying[0][0]] if flying else []
        if preps:
            nxt.append(preps[0][1])
        now = max(now, min(nxt))
    if chunks is None:
        every = [(dz, color) for dz in range(NZ) for color in range(COLORS)]
        return sorted(every, key=lambda t: max(arrived.get(q, 0.0) for q in pieces_of_chunk(*t)))
    return steps, now


PREPS = (
    [(("limits", 0), 0.2, 0.3), (("places", 0), 0.8, 0.4)]
    + [(("own", k), 3.0, 0.3) for k in range(2)]
    + [(("other", k), 11.0, 0.3) for k in range(2)]
    + [(("mask", 0), 16.0, 0.1), (("mask", 1), 32.0, 0.1)]
)
CHUNKS = plan(PREPS)
STEPS, _ = plan(PREPS, CHUNKS)
SPOT = {chunk: k for k, chunk in enumerate(CHUNKS)}
TRANSFERS = [s[3] for s in STEPS if s[0] == "send"]


def shared_semaphores(steps):
    sent = {s[3]: k for k, s in enumerate(steps) if s[0] == "send"}
    waited = {s[1]: k for k, s in enumerate(steps) if s[0] == "wait"}
    links = {}
    for s in steps:
        if s[0] == "send":
            links.setdefault(s[1:3], []).append(s[3])
    number, count = {}, 0
    for (axis, m), queue in links.items():
        slots = []
        for q in queue:
            for slot in slots:
                if any(sent[r] > waited[slot[1]] and waited[r] < sent[q] for r in links[axis, -m]):
                    break
            else:
                slot = [count, None]
                slots.append(slot)
                count += 1
            slot[1] = q
            number[q] = slot[0]
    return number, count


NUMBER, SEMAPHORES = shared_semaphores(STEPS)
LARGE = [q for q in TRANSFERS if q[:2] in (("A", "z"), ("B", "x"), ("C", "y"))]
SMALL = [q for q in TRANSFERS if q not in LARGE]
WHOLE = len(SMALL) // 4 * 4
GROUP = {q: 0 for q in LARGE}
GROUP.update({q: 1 if k < WHOLE else 2 + k - WHOLE for k, q in enumerate(SMALL)})


def merge(parts):
    peak = parts[0][0]
    for p in parts[1:]:
        peak = jnp.maximum(peak, p[0])
    total = jnp.zeros_like(peak)
    moment = jnp.zeros_like(peak)
    for m, t, mo in parts:
        shift = m - peak
        ratio = jnp.exp(shift)
        total = total + ratio * t
        moment = moment + ratio * (mo + t * shift)
    return peak, total, moment


def kernel(hid_ref, lm_ref, pos_ref, lim_ref, mask_ref, ent_ref, mean_ref,
           held, weight, stage, hstage, pstage, logits, small, mask_in, table, lim_win, pos_col,
           wstat, stat, from_z, plane, from_plane, ents, masks,
           send_sem, recv_sem, hx_sem, w_sem, mz_sem, my_sem, rz_sem, rp_sem, re_sem, copy_sem):
    z, y, x, c = (lax.axis_index(a) for a in AXES)
    here = {"z": z, "y": y, "x": x, "c": c}

    def device(**moved):
        return tuple(lax.rem(here[a] + moved[a], SIZE[a]) if a in moved and a != "c" else
                     (1 - c if a in moved else here[a]) for a in AXES)

    own_w = pltpu.make_async_copy(lm_ref, stage.at[0], copy_sem.at[0])
    own_h = pltpu.make_async_copy(hid_ref, hstage, copy_sem.at[1])
    own_h.start()
    own_w.start()
    given = [pltpu.make_async_copy(lim_ref, small.at[0], copy_sem.at[2]),
             pltpu.make_async_copy(pos_ref, small.at[1], copy_sem.at[3]),
             pltpu.make_async_copy(mask_ref, mask_in, copy_sem.at[4])]
    for copy in given:
        copy.start()

    barrier = pltpu.get_barrier_semaphore()
    near = [device(**{a: d}) for a in "zyx" for d in (1, SIZE[a] - 1)] + [device(c=1)]
    for who in near:
        pl.semaphore_signal(barrier, inc=1, device_id=who, device_id_type=MESH)
    with jax.named_scope("T_barrier"):
        pl.semaphore_wait(barrier, len(near))

    with jax.named_scope("T_ownh"):
        own_h.wait()
    swap = pltpu.make_async_remote_copy(
        src_ref=hstage.at[pl.ds(pl.multiple_of((1 - c) * HALF, RB), HALF), :], dst_ref=pstage,
        send_sem=hx_sem.at[0], recv_sem=hx_sem.at[1], device_id=device(c=1), device_id_type=MESH)
    swap.start()
    give_w = pltpu.make_async_remote_copy(
        src_ref=lm_ref, dst_ref=stage.at[1],
        send_sem=w_sem.at[0], recv_sem=w_sem.at[1], device_id=device(c=1), device_id_type=MESH)

    def feature(dx):
        return pl.ds(pl.multiple_of(lax.rem(x + dx, NX) * FEAT, 128), FEAT)

    mine = hstage[pl.ds(pl.multiple_of(c * HALF, RB), HALF), :].astype(jnp.float32)
    with jax.named_scope("T_swap"):
        swap.wait_recv()
    theirs = pstage[...].astype(jnp.float32)
    first = c == 0
    left = jnp.where(first, mine, theirs)
    right = jnp.where(first, theirs, mine)
    both = jnp.concatenate([left, right], axis=1).astype(jnp.bfloat16)
    for k in range(COLORS):
        held[pl.ds(SPOT[0, k] * CHUNK, RB), feature(0)] = both[k * RB:(k + 1) * RB]

    def rows_of(p):
        color, axis = "ABC".index(p[0]), p[1]
        dz = window_of(p)
        if p[:2] == ("B", "x"):
            return pl.ds(SPOT[dz, color] * CHUNK, CHUNK)
        if axis == "z":
            dy = p[3] if color == 0 else 0
        elif axis == "y":
            dy = p[2] if color == 0 else p[3]
        else:
            dy = p[2] if color == 0 else 0
        return pl.ds(SPOT[dz, color] * CHUNK + dy * RB, RB)

    def place(p):
        if p[:2] in (("A", "z"), ("C", "y")):
            return held.at[rows_of(p), :]
        return held.at[rows_of(p), feature(p[-1] if p[1] == "x" else 0)]

    def transfer(q, axis, m):
        n = SIZE[axis]
        if axis == "x":
            src = dst = held.at[rows_of(q), feature(q[-1] + m + NX)]
        else:
            at = {("A", "y"): 2, ("A", "z"): 2, ("B", "z"): 2, ("C", "z"): 2}.get(q[:2], 3)
            src = place(q[:at] + ((q[at] + m) % n,) + q[at + 1:])
            dst = place(q)
        return pltpu.make_async_remote_copy(
            src_ref=src, dst_ref=dst, send_sem=send_sem.at[GROUP[q]], recv_sem=recv_sem.at[NUMBER[q]],
            device_id=device(**{axis: m % n}), device_id_type=MESH)

    started = {}
    lanes = lax.broadcasted_iota(jnp.int32, (128, 128), 1)

    lane_of = lax.broadcasted_iota(jnp.int32, (8, LANES), 1)
    lane_chunk = lane_of // CHUNK

    def limits():
        for copy in given:
            copy.wait()
        masks[0, 0] = jnp.zeros((1, 128), jnp.float32)
        masks[0, 0, :, 0:TOK] = mask_in[...].astype(jnp.float32)
        row = lax.broadcasted_iota(jnp.int32, (3 * 128, LANES), 0)
        column = lax.broadcasted_iota(jnp.int32, (3 * 128, LANES), 1)
        color, dy, i = column // CHUNK, column % CHUNK // RB, column % RB
        want = lax.rem(y + dy, NY) * TOK + c * HALF + color * RB + i
        pick = jnp.where((row == want) & (color < COLORS), 1.0, 0.0).astype(jnp.bfloat16)
        for k in range(2):
            given_rows = jnp.concatenate(
                [small[k, pl.ds(j, NZ, stride=3), :] for j in range(3)], axis=1)
            found = jnp.zeros((NZ, LANES), jnp.float32)
            for shift in (14, 7, 0):
                digit = lax.bitwise_and(lax.shift_right_logical(given_rows, shift), 127)
                digit = digit.astype(jnp.float32).astype(jnp.bfloat16)
                found = found * 128.0 + jnp.dot(digit, pick, preferred_element_type=jnp.float32)
            table[k] = found

    def places():
        for w in range(WINDOWS):
            line = jnp.zeros((8, LANES), jnp.float32)
            for j in range(4):
                dz, color = CHUNKS[4 * w + j]
                source = jnp.broadcast_to(table[0, pl.ds(lax.rem(z + dz, NZ), 1), :], (8, LANES))
                if j != color:
                    source = pltpu.roll(source, (j - color) * CHUNK % LANES, 1)
                line = jnp.where(lane_chunk == j, source, line)
            lim_win[w] = line[0:1].astype(jnp.int32)
        pos_col[...] = jnp.broadcast_to(table[1, pl.ds(z, 1), :], (128, LANES)).T

    def settle(which, k):
        def one(r, carry):
            at = pl.ds(pl.multiple_of(r * 256, 128), 256)
            weight[which, 0:WID, at] = stage[which, :, at]
            return carry

        lax.fori_loop(7 * k, 7 * k + 7, one, 0)

    def mask_z(dz):
        return pltpu.make_async_remote_copy(
            src_ref=masks.at[0, 0], dst_ref=masks.at[8 - dz, 0], send_sem=mz_sem.at[0],
            recv_sem=mz_sem.at[1], device_id=device(z=dz), device_id_type=MESH)

    def mask_y(dy):
        return pltpu.make_async_remote_copy(
            src_ref=masks.at[:, 0], dst_ref=masks.at[:, 4 - dy], send_sem=my_sem.at[0],
            recv_sem=my_sem.at[1], device_id=device(y=dy), device_id_type=MESH)

    def whole(ref, sems):
        return pltpu.make_async_remote_copy(
            src_ref=ref, dst_ref=ref, send_sem=sems.at[0], recv_sem=sems.at[1],
            device_id=device(z=1), device_id_type=MESH)

    all_mask_z = whole(masks.at[1:NZ, 0], mz_sem)
    all_mask_y = whole(masks.at[:, 1:NY], my_sem)
    all_stat = whole(from_z.at[1:NZ], rz_sem)
    all_plane = whole(from_plane.at[1:NY * NX], rp_sem)
    all_ents = whole(ents.at[1:2 * NZ], re_sem)

    def prep(name, k):
        if name == "limits":
            limits()
        elif name == "places":
            places()
        elif name == "own":
            if k == 0:
                own_w.wait()
            settle(0, k)
        elif name == "other":
            if k == 0:
                give_w.wait_recv()
            settle(1, k)
        elif k == 0:
            for dz in range(1, NZ):
                mask_z(dz).start()
        else:
            all_mask_z.wait_recv()
            for dy in range(1, NY):
                mask_y(dy).start()

    number = (z * NY + y) * (2 * NX) + x * 2
    starts = ((number + c) * WID, (number + 1 - c) * WID)
    depth = lax.broadcasted_iota(jnp.int32, (PAD, LANES), 0)

    def multiply(w, slot):
        for k in range(2):
            logits[slot, k] = lax.dot_general(
                weight[k], held[w * LANES:(w + 1) * LANES, :], (((1,), (1,)), ((), ())),
                preferred_element_type=jnp.float32)

    def reduce_rows(w, slot):
        limit = lim_win[w]
        peak = jnp.full((1, LANES), NEG, jnp.float32)
        for k in range(2):
            bound = jnp.minimum(limit - starts[k], WID)
            logits[slot, k] = jnp.where(depth < bound, logits[slot, k], NEG)
            peak = jnp.maximum(peak, jnp.max(logits[slot, k], axis=0, keepdims=True))
        total = jnp.zeros((1, LANES), jnp.float32)
        moment = jnp.zeros((1, LANES), jnp.float32)
        for k in range(2):
            shifted = logits[slot, k] - peak
            e = jnp.exp(shifted)
            total = total + jnp.sum(e, axis=0, keepdims=True)
            moment = moment + jnp.sum(e * shifted, axis=0, keepdims=True)
        wstat[w] = jnp.concatenate([peak, total, moment, jnp.zeros((5, LANES), jnp.float32)], axis=0)
        reduced.append(w)
        for dz in range(NZ):
            spots = [SPOT[dz, color] for color in range(COLORS)]
            if any(spot // 4 == w for spot in spots) and all(spot // 4 in reduced for spot in spots):
                line = jnp.zeros((8, LANES), jnp.float32)
                for color, spot in enumerate(spots):
                    source = wstat[spot // 4]
                    if spot % 4 != color:
                        source = pltpu.roll(source, (color - spot % 4) * CHUNK % LANES, 1)
                    line = jnp.where(lane_chunk == color, source, line)
                for k in range(3):
                    stat[dz, k] = line[k:k + 1]
                if dz:
                    stat_copy(dz).start()

    def stat_copy(dz):
        return pltpu.make_async_remote_copy(
            src_ref=stat.at[dz], dst_ref=from_z.at[8 - dz], send_sem=rz_sem.at[0],
            recv_sem=rz_sem.at[1], device_id=device(z=dz), device_id_type=MESH)

    done, reduced = [], []

    def window(dz):
        if done:
            reduce_rows(done[-1], len(done) % 2)
        if dz is None:
            return
        done.append(dz)
        multiply(dz, len(done) % 2)

    first_send = True
    for step in STEPS:
        if step[0] == "send":
            _, axis, m, q = step
            started[q] = transfer(q, axis, m)
            started[q].start()
        else:
            if first_send:
                give_w.start()
                first_send = False
            if step[0] == "wait":
                started[step[1]].wait_recv()
            elif step[0] == "prep":
                prep(*step[1])
            else:
                window(step[1])
    with jax.named_scope("T_last"):
        window(None)

    with jax.named_scope("T_zround"):
        all_stat.wait_recv()
    parts = [tuple(stat[0, k] for k in range(3))]
    parts += [tuple(from_z[dz, k] for k in range(3)) for dz in range(1, NZ)]
    merged = merge(parts)
    for k in range(3):
        plane[k] = merged[k]

    spots = [(dy, dx) for dy in range(NY) for dx in range(NX) if dy or dx]

    def plane_copy(dy, dx):
        back = (NY - dy) % NY * NX + (NX - dx) % NX
        return pltpu.make_async_remote_copy(
            src_ref=plane, dst_ref=from_plane.at[back], send_sem=rp_sem.at[0],
            recv_sem=rp_sem.at[1], device_id=device(y=dy, x=dx), device_id_type=MESH)

    for dy, dx in spots:
        plane_copy(dy, dx).start()
    all_mask_y.wait_recv()
    with jax.named_scope("T_planeround"):
        all_plane.wait_recv()
    groups = []
    for dy in range(NY):
        parts = [tuple(from_plane[dy * NX + dx, k] for k in range(3)) for dx in range(NX) if dy or dx]
        group = merge(parts if dy else [merged] + parts)
        if dy:
            lines = jnp.concatenate([*group, jnp.zeros((5, LANES), jnp.float32)], axis=0)
            ahead = pltpu.roll(lines, dy * RB, 1)
            around = pltpu.roll(lines, (dy * RB - CHUNK) % LANES, 1)
            lines = jnp.where(lane_of % CHUNK >= dy * RB, ahead, around)
            group = tuple(lines[k:k + 1] for k in range(3))
        groups.append(group)
    peak, total, moment = merge(groups)
    entropy = jnp.log(total) - moment / total

    masked = jnp.zeros((1, 128), jnp.float32)
    found = []
    column = jnp.broadcast_to(entropy, (128, LANES)).T[:COLORS * CHUNK]
    for k in range(2):
        owner = jnp.where(c == 0, 2 * z + k, 31 - 2 * z - k)
        line = lanes[:1]
        spot = jnp.where(line < TOK, owner * TOK + line, -1).astype(jnp.float32)
        here_e = jnp.where(pos_col[0:COLORS * CHUNK, :] == spot, column, 0.0)
        here_e = jnp.sum(here_e, axis=0, keepdims=True)
        found.append(here_e)
        dz = lax.rem(owner // NY - z + NZ, NZ)
        dy = lax.rem(lax.rem(owner, NY) - y + NY, NY)
        masked = masked + here_e * masks[dz, dy]
    masked = jnp.sum(masked, axis=1, keepdims=True)
    lane = lanes[:1]
    for k in range(2):
        ents[0, k] = jnp.where(lane < TOK, found[k], masked if k == 0 else 0.0)

    others = [(dz, other) for dz in range(NZ) for other in range(2) if dz or other]

    def ent_copy(dz, other):
        target = device(z=dz, c=1) if other else device(z=dz)
        return pltpu.make_async_remote_copy(
            src_ref=ents.at[0], dst_ref=ents.at[(NZ - dz) % NZ * 2 + other], send_sem=re_sem.at[0],
            recv_sem=re_sem.at[1], device_id=target, device_id_type=MESH)

    for dz, other in others:
        ent_copy(dz, other).start()

    started_count = jnp.sum(jnp.sum(masks[...].reshape(NZ * NY, 128), axis=0, keepdims=True), axis=1, keepdims=True)
    for group, rows in ((0, len(LARGE) * RB), (1, WHOLE // 4 * RB)):
        pltpu.make_async_remote_copy(
            src_ref=held.at[0:rows, :], dst_ref=held.at[0:rows, :], send_sem=send_sem.at[group],
            recv_sem=recv_sem.at[0], device_id=device(z=1), device_id_type=MESH).wait_send()
    for q in SMALL[WHOLE:]:
        started[q].wait_send()
    swap.wait_send()
    give_w.wait_send()
    all_mask_z.wait_send()
    all_mask_y.wait_send()
    all_stat.wait_send()
    all_plane.wait_send()

    with jax.named_scope("T_entround"):
        all_ents.wait_recv()
    total_masked = jnp.sum(ents[:, 0].reshape(2 * NZ, 128), axis=0, keepdims=True)
    total_masked = jnp.sum(jnp.where(lane == TOK, total_masked, 0.0), axis=1, keepdims=True)
    mean = total_masked / jnp.maximum(started_count, 1.0)
    mean_ref[...] = jnp.broadcast_to(mean, (1, 128))
    mine_s = z * NY + y
    index = jnp.where(z < NZ // 2, mine_s, 31 - mine_s)
    dz = lax.rem(index // 2 - z + NZ, NZ)
    other = jnp.where(z < NZ // 2, c, 1 - c)
    ent_ref[...] = ents[dz * 2 + other, lax.rem(index, 2)][:, 0:TOK]
    all_ents.wait_send()


def local(hidden, lm_head, positions, vocab_limits, loss_mask):
    f32, bf16 = jnp.float32, jnp.bfloat16
    dma = pltpu.SemaphoreType.DMA
    any_space = pl.BlockSpec(memory_space=pl.ANY)
    vmem = pl.BlockSpec(memory_space=pltpu.VMEM)
    ent, mean = pl.pallas_call(
        kernel,
        out_shape=(jax.ShapeDtypeStruct((1, TOK), f32), jax.ShapeDtypeStruct((1, 128), f32)),
        in_specs=[any_space] * 5,
        out_specs=(vmem, vmem),
        scratch_shapes=[
            pltpu.VMEM((NZ * COLORS * CHUNK, D), bf16),
            pltpu.VMEM((2, PAD, D), bf16),
            pltpu.VMEM((2, WID, D), bf16),
            pltpu.VMEM((TOK, FEAT // 2), bf16),
            pltpu.VMEM((HALF, FEAT // 2), bf16),
            pltpu.VMEM((2, 2, PAD, LANES), f32),
            pltpu.VMEM((2, 24, 128), jnp.int32),
            pltpu.VMEM((1, TOK), jnp.int32),
            pltpu.VMEM((2, NZ, LANES), f32),
            pltpu.VMEM((WINDOWS, 1, LANES), jnp.int32),
            pltpu.VMEM((LANES, 128), f32),
            pltpu.VMEM((WINDOWS, 8, LANES), f32),
            pltpu.VMEM((NZ, 3, 1, 256), f32),
            pltpu.VMEM((NZ, 3, 1, 256), f32),
            pltpu.VMEM((3, 1, 256), f32),
            pltpu.VMEM((NY * NX, 3, 1, 256), f32),
            pltpu.VMEM((2 * NZ, 2, 1, 128), f32),
            pltpu.VMEM((NZ, NY, 1, 128), f32),
            dma((2 + len(SMALL) - WHOLE,)), dma((SEMAPHORES,)), *[dma((2,))] * 7, dma((5,)),
        ],
        compiler_params=pltpu.CompilerParams(
            collective_id=0, has_side_effects=True, vmem_limit_bytes=62 * 2**20),
    )(hidden, lm_head.T, positions.reshape(24, 128), vocab_limits.reshape(24, 128), loss_mask.reshape(1, TOK))
    return ent.reshape(TOK), mean[0, 0]


def solution(mesh):
    torus = Mesh(mesh.devices.reshape(NZ, NY, NX, 2), AXES)
    in_specs = (P(("z", "y"), ("x", "c")), P(None, AXES), P(), P(), P(("z", "y")))
    return jax.shard_map(local, mesh=torus, in_specs=in_specs, out_specs=(P(("z", "y")), P()), check_vma=False)
```

time: 85.5 us -> 81.2 us (0.950)
  Pallas kernels: 81.9 us -> 77.6 us
    pallas_call x1, Pallas kernels: 81.9 us -> 77.6 us  [local(): pl.pallas_call(kernel, out_shape=(jax.ShapeDtypeStruct((1, TOK), f32), ja...]
where the time goes in v3:
time: 81.2 us; the launch traced here: 81.1 us
  Pallas kernels  77.6 us (96%)
  between operations  2.4 us (3%)
  local copies, waits for them, and re-layouts  1.11 us (1%)
    pallas_call x1, Pallas kernels, local(): pl.pallas_call(kernel, out_shape=(jax.ShapeDtypeStruct((1, TOK), f32), ja...  77.6 us

profile of v3, /device:TPU:1, one launch (start us, length us, event | category | flops | bytes accessed | tf_op | source)
XLA Modules:
  0.0 81.1 jit_solution(302838800180809339)
XLA Ops:
  0.6 77.6 %shard_map.68 = (f32[1,96]{1,0:T(1,128)}, f32[1,128]{1,0:T(1,128)}) custom-call(bf16[96,448]{1,0:T(8,128)(2,1)} %hid_ref.1, bf16[594,3584]{1,0:T(8,128)(2,1)} %bitcast.7, s32[24,128]{1,0:T(8,128)} %bitcast.8, s32[24,128]{1,0:T(8,128)} %bitcast.9, s32[1,96]{1,0:T(1,128)} %bitcast.10), custom_call_target="tpu_custom_call" | custom-call | tf_op jit(solution)/shard_map/pallas_call | solution.py:592
  78.2 1.1 %copy.9 = f32[96]{0:T(128)} copy(f32[96]{0:T(128)} %bitcast.12) | data formatting | bytes 768

commit v4 on v3

--- a/solution.py
+++ b/solution.py
@@ -20,16 +20,16 @@
 WINDOWS = NZ * COLORS * CHUNK // LANES
 NEG = -1e30
 DEADLINE = (
-    (18.1, 16.1, 16.7),
-    (19.9, 17.9, 18.5),
-    (23.9, 21.9, 22.5),
-    (24.8, 22.8, 23.4),
-    (26.9, 24.9, 25.5),
-    (24.1, 22.1, 22.7),
-    (24.2, 22.2, 22.8),
-    (23.8, 21.8, 22.4),
+    (3.9, -0.7, 0.5),
+    (12.3, 9.6, 12.3),
+    (17.2, 16.7, 14.0),
+    (16.6, 15.8, 16.5),
+    (21.7, 22.0, 23.4),
+    (12.3, 23.1, 18.4),
+    (15.1, 15.7, 15.8),
+    (12.2, 15.3, 13.4),
 )
-UNIT, HOP, BACKLOG = 0.615, 1.75, 1.5
+UNIT, HOP, BACKLOG = 0.615, 2.5, 2
 WINDOW = 3.05
 
 
@@ -333,6 +333,7 @@
     started = {}
     lanes = lax.broadcasted_iota(jnp.int32, (128, 128), 1)
 
+    rows_z = lax.rem(z + NZ // 2, NZ)
     lane_of = lax.broadcasted_iota(jnp.int32, (8, LANES), 1)
     lane_chunk = lane_of // CHUNK
 
@@ -366,7 +367,7 @@
                     source = pltpu.roll(source, (j - color) * CHUNK % LANES, 1)
                 line = jnp.where(lane_chunk == j, source, line)
             lim_win[w] = line[0:1].astype(jnp.int32)
-        pos_col[...] = jnp.broadcast_to(table[1, pl.ds(z, 1), :], (128, LANES)).T
+        pos_col[...] = jnp.broadcast_to(table[1, pl.ds(rows_z, 1), :], (128, LANES)).T
 
     def settle(which, k):
         def one(r, carry):
@@ -455,13 +456,14 @@
                     line = jnp.where(lane_chunk == color, source, line)
                 for k in range(3):
                     stat[dz, k] = line[k:k + 1]
-                if dz:
+                if dz != NZ // 2:
                     stat_copy(dz).start()
 
     def stat_copy(dz):
+        ahead = (dz + NZ // 2) % NZ
         return pltpu.make_async_remote_copy(
-            src_ref=stat.at[dz], dst_ref=from_z.at[8 - dz], send_sem=rz_sem.at[0],
-            recv_sem=rz_sem.at[1], device_id=device(z=dz), device_id_type=MESH)
+            src_ref=stat.at[dz], dst_ref=from_z.at[NZ - ahead], send_sem=rz_sem.at[0],
+            recv_sem=rz_sem.at[1], device_id=device(z=ahead), device_id_type=MESH)
 
     done, reduced = [], []
 
@@ -494,7 +496,7 @@
 
     with jax.named_scope("T_zround"):
         all_stat.wait_recv()
-    parts = [tuple(stat[0, k] for k in range(3))]
+    parts = [tuple(stat[NZ // 2, k] for k in range(3))]
     parts += [tuple(from_z[dz, k] for k in range(3)) for dz in range(1, NZ)]
     merged = merge(parts)
     for k in range(3):
@@ -531,7 +533,7 @@
     found = []
     column = jnp.broadcast_to(entropy, (128, LANES)).T[:COLORS * CHUNK]
     for k in range(2):
-        owner = jnp.where(c == 0, 2 * z + k, 31 - 2 * z - k)
+        owner = jnp.where(c == 0, 2 * rows_z + k, 31 - 2 * rows_z - k)
         line = lanes[:1]
         spot = jnp.where(line < TOK, owner * TOK + line, -1).astype(jnp.float32)
         here_e = jnp.where(pos_col[0:COLORS * CHUNK, :] == spot, column, 0.0)
@@ -578,7 +580,7 @@
     mean_ref[...] = jnp.broadcast_to(mean, (1, 128))
     mine_s = z * NY + y
     index = jnp.where(z < NZ // 2, mine_s, 31 - mine_s)
-    dz = lax.rem(index // 2 - z + NZ, NZ)
+    dz = lax.rem(index // 2 + NZ // 2 - z + NZ, NZ)
     other = jnp.where(z < NZ // 2, c, 1 - c)
     ent_ref[...] = ents[dz * 2 + other, lax.rem(index, 2)][:, 0:TOK]
     all_ents.wait_send()

time: 81.2 us -> 78.3 us (0.964)
  Pallas kernels: 77.6 us -> 74.7 us
    pallas_call x1, Pallas kernels: 77.6 us -> 74.7 us  [local(): pl.pallas_call(kernel, out_shape=(jax.ShapeDtypeStruct((1, TOK), f32), ja...]
where the time goes in v4:
time: 78.3 us; the launch traced here: 78.2 us
  Pallas kernels  74.7 us (95%)
  between operations  2.4 us (3%)
  local copies, waits for them, and re-layouts  1.11 us (1%)
    pallas_call x1, Pallas kernels, local(): pl.pallas_call(kernel, out_shape=(jax.ShapeDtypeStruct((1, TOK), f32), ja...  74.7 us

profile of v4, /device:TPU:1, one launch (start us, length us, event | category | flops | bytes accessed | tf_op | source)
XLA Modules:
  0.0 78.2 jit_solution(16494251932309947880)
XLA Ops:
  0.6 74.7 %shard_map.68 = (f32[1,96]{1,0:T(1,128)}, f32[1,128]{1,0:T(1,128)}) custom-call(bf16[96,448]{1,0:T(8,128)(2,1)} %hid_ref.1, bf16[594,3584]{1,0:T(8,128)(2,1)} %bitcast.7, s32[24,128]{1,0:T(8,128)} %bitcast.8, s32[24,128]{1,0:T(8,128)} %bitcast.9, s32[1,96]{1,0:T(1,128)} %bitcast.10), custom_call_target="tpu_custom_call" | custom-call | tf_op jit(solution)/shard_map/pallas_call | solution.py:594
  75.3 1.1 %copy.9 = f32[96]{0:T(128)} copy(f32[96]{0:T(128)} %bitcast.12) | data formatting | bytes 768

commit v5 on v4

--- a/solution.py
+++ b/solution.py
@@ -20,16 +20,17 @@
 WINDOWS = NZ * COLORS * CHUNK // LANES
 NEG = -1e30
 DEADLINE = (
-    (3.9, -0.7, 0.5),
-    (12.3, 9.6, 12.3),
-    (17.2, 16.7, 14.0),
-    (16.6, 15.8, 16.5),
-    (21.7, 22.0, 23.4),
-    (12.3, 23.1, 18.4),
-    (15.1, 15.7, 15.8),
-    (12.2, 15.3, 13.4),
+    (-18.7, -45.5, 48.4),
+    (-28.8, 7.7, -36.2),
+    (72.7, 12.8, 9.8),
+    (-33.4, 28.9, 15.4),
+    (-4.9, 31.5, 18.3),
+    (10.5, 12.3, -3.5),
+    (-36.7, 12.9, 18.2),
+    (79.1, 7.0, 5.2),
 )
-UNIT, HOP, BACKLOG = 0.615, 2.5, 2
+UNIT, HOP, BACKLOG = 0.615, 2.5, 1.5
+DEEP = 3.5
 WINDOW = 3.05
 
 
@@ -131,10 +132,11 @@
             heapq.heappush(waiting[axis, m], (latest(q) - size * UNIT, count, size, q))
             count += 1
 
-    def pump():
+    def pump(ahead=None):
         nonlocal count
+        ahead = BACKLOG if ahead is None else ahead
         for link in free:
-            while waiting[link] and free[link] - now < BACKLOG:
+            while waiting[link] and free[link] - now < ahead:
                 _, _, size, q = heapq.heappop(waiting[link])
                 free[link] = max(free[link], now) + size * UNIT
                 heapq.heappush(flying, (free[link] + HOP, count, q))
@@ -176,6 +178,7 @@
         ready = [] if blocked() else [w for w in left if all(
             q in have for chunk in chunks[4 * w:4 * w + 4] for q in pieces_of_chunk(*chunk))]
         if ready:
+            pump(DEEP)
             steps.append(("window", ready[0]))
             left.remove(ready[0])
             now += WINDOW
@@ -285,6 +288,7 @@
     give_w = pltpu.make_async_remote_copy(
         src_ref=lm_ref, dst_ref=stage.at[1],
         send_sem=w_sem.at[0], recv_sem=w_sem.at[1], device_id=device(c=1), device_id_type=MESH)
+    give_w.start()
 
     def feature(dx):
         return pl.ds(pl.multiple_of(lax.rem(x + dx, NX) * FEAT, 128), FEAT)
@@ -434,12 +438,13 @@
         peak = jnp.full((1, LANES), NEG, jnp.float32)
         for k in range(2):
             bound = jnp.minimum(limit - starts[k], WID)
-            logits[slot, k] = jnp.where(depth < bound, logits[slot, k], NEG)
-            peak = jnp.maximum(peak, jnp.max(logits[slot, k], axis=0, keepdims=True))
+            allowed = jnp.where(depth < bound, logits[slot, k], NEG)
+            peak = jnp.maximum(peak, jnp.max(allowed, axis=0, keepdims=True))
         total = jnp.zeros((1, LANES), jnp.float32)
         moment = jnp.zeros((1, LANES), jnp.float32)
         for k in range(2):
-            shifted = logits[slot, k] - peak
+            bound = jnp.minimum(limit - starts[k], WID)
+            shifted = jnp.where(depth < bound, logits[slot, k], NEG) - peak
             e = jnp.exp(shifted)
             total = total + jnp.sum(e, axis=0, keepdims=True)
             moment = moment + jnp.sum(e * shifted, axis=0, keepdims=True)
@@ -475,16 +480,12 @@
         done.append(dz)
         multiply(dz, len(done) % 2)
 
-    first_send = True
     for step in STEPS:
         if step[0] == "send":
             _, axis, m, q = step
             started[q] = transfer(q, axis, m)
             started[q].start()
         else:
-            if first_send:
-                give_w.start()
-                first_send = False
             if step[0] == "wait":
                 started[step[1]].wait_recv()
             elif step[0] == "prep":

time: 78.3 us -> 78.1 us (level)
  no operation moved by 1% of the time
where the time goes in v5:
time: 78.1 us; the launch traced here: 78 us
  Pallas kernels  74.4 us (95%)
  between operations  2.4 us (3%)
  local copies, waits for them, and re-layouts  1.11 us (1%)
    pallas_call x1, Pallas kernels, local(): pl.pallas_call(kernel, out_shape=(jax.ShapeDtypeStruct((1, TOK), f32), ja...  74.4 us

profile of v5, /device:TPU:1, one launch (start us, length us, event | category | flops | bytes accessed | tf_op | source)
XLA Modules:
  0.0 78.0 jit_solution(13887132515551966049)
XLA Ops:
  0.6 74.4 %shard_map.68 = (f32[1,96]{1,0:T(1,128)}, f32[1,128]{1,0:T(1,128)}) custom-call(bf16[96,448]{1,0:T(8,128)(2,1)} %hid_ref.1, bf16[594,3584]{1,0:T(8,128)(2,1)} %bitcast.7, s32[24,128]{1,0:T(8,128)} %bitcast.8, s32[24,128]{1,0:T(8,128)} %bitcast.9, s32[1,96]{1,0:T(1,128)} %bitcast.10), custom_call_target="tpu_custom_call" | custom-call | tf_op jit(solution)/shard_map/pallas_call | solution.py:595
  75.1 1.1 %copy.9 = f32[96]{0:T(128)} copy(f32[96]{0:T(128)} %bitcast.12) | data formatting | bytes 768
